TPU v7x, 16 devices: a whole 2x2x2 slice. The times are simulated.
16 devices in a mesh: dp: 2 (over z), col: 2 (over y), fsdp: 4 (over x, core).
Axes of the slice: x: 2, y: 2, z: 2, core: 2. Of those that a mesh axis runs over, the one named last changes fastest.
Arguments:
- x_act: bfloat16 [65536, 960], P(('dp', 'col', 'fsdp'))
- dy_out: bfloat16 [65536, 960], P(('dp', 'col', 'fsdp'))
- w_gate: bfloat16 [960, 2560], P(None, ('col', 'fsdp'))
- w_up: bfloat16 [960, 2560], P(None, ('col', 'fsdp'))
- w_down: bfloat16 [2560, 960], P(('col', 'fsdp'))
- v_gate: bfloat16 [960, 2560], P(None, ('col', 'fsdp'))
- v_up: bfloat16 [960, 2560], P(None, ('col', 'fsdp'))
- v_down: bfloat16 [2560, 960], P(('col', 'fsdp'))
- g_next: float32 [16, 3, 960, 2560], P(('dp', 'col', 'fsdp'))
Outputs:
- output 1: bfloat16 [65536, 960], P(('dp', 'col', 'fsdp'))
- output 2: float32 [3, 960, 2560], P(None, None, ('col', 'fsdp'))
- output 3: float32 [16, 3, 960, 2560], P(('dp', 'col', 'fsdp'))
- output 4: bfloat16 [960, 2560], replicated
- output 5: bfloat16 [960, 2560], replicated
- output 6: bfloat16 [2560, 960], replicated
All inputs are finite; a program needn't handle non-finite values.
Results may differ from a plain program's by a relative error of at most 0.0105823.
Values are sent between devices in bfloat16 or wider.
A program may use at most 1 GiB of HBM per device.

v0:
```python
import jax
import jax.numpy as jnp
from jax import lax
from jax.sharding import PartitionSpec as P

ALL_AXES = ('dp', 'col', 'fsdp')
FSDP_AXES = ('col', 'fsdp')


def local_backward(x_loc, dy_loc, gate_full, up_full, down_full):
    pre_gate = jnp.dot(x_loc, gate_full, preferred_element_type=jnp.float32)
    pre_up = jnp.dot(x_loc, up_full, preferred_element_type=jnp.float32)
    sig_gate = jax.nn.sigmoid(pre_gate)
    act_gate = pre_gate * sig_gate
    hidden = (act_gate * pre_up).astype(jnp.bfloat16)
    d_hidden = jnp.einsum('td,fd->tf', dy_loc, down_full, preferred_element_type=jnp.float32)
    d_gate = (d_hidden * pre_up * sig_gate * (1.0 + pre_gate * (1.0 - sig_gate))).astype(jnp.bfloat16)
    d_up = (d_hidden * act_gate).astype(jnp.bfloat16)
    dx_loc = (jnp.einsum('tf,df->td', d_gate, gate_full, preferred_element_type=jnp.float32)
              + jnp.einsum('tf,df->td', d_up, up_full, preferred_element_type=jnp.float32)).astype(jnp.bfloat16)
    grad_local = jnp.stack([
        jnp.einsum('td,tf->df', x_loc, d_gate, preferred_element_type=jnp.float32),
        jnp.einsum('td,tf->df', x_loc, d_up, preferred_element_type=jnp.float32),
        jnp.einsum('td,tf->df', dy_loc, hidden, preferred_element_type=jnp.float32),
    ])
    return dx_loc, grad_local


def solution(mesh):
    def device_step(x_loc, dy_loc, w_gate, w_up, w_down, v_gate, v_up, v_down, g_next):
        gate_full = lax.all_gather(w_gate, FSDP_AXES, axis=1, tiled=True)
        up_full = lax.all_gather(w_up, FSDP_AXES, axis=1, tiled=True)
        down_full = lax.all_gather(w_down, FSDP_AXES, axis=0, tiled=True)
        v_gate_full = lax.all_gather(v_gate, FSDP_AXES, axis=1, tiled=True)
        v_up_full = lax.all_gather(v_up, FSDP_AXES, axis=1, tiled=True)
        v_down_full = lax.all_gather(v_down, FSDP_AXES, axis=0, tiled=True)
        grad_shard = lax.psum_scatter(g_next[0].astype(jnp.bfloat16), FSDP_AXES, scatter_dimension=2, tiled=True)
        grad_next = lax.psum(grad_shard.astype(jnp.float32), 'dp')
        dx_loc, grad_local = local_backward(x_loc, dy_loc, gate_full, up_full, down_full)
        return dx_loc, grad_next, grad_local[None], v_gate_full, v_up_full, v_down_full

    row_spec = P(ALL_AXES, None)
    col_shard = P(None, FSDP_AXES)
    row_shard = P(FSDP_AXES, None)
    dev_spec = P(ALL_AXES, None, None, None)
    return jax.shard_map(
        device_step, mesh=mesh,
        in_specs=(row_spec, row_spec, col_shard, col_shard, row_shard, col_shard, col_shard, row_shard, dev_spec),
        out_specs=(row_spec, P(None, None, FSDP_AXES), dev_spec, P(), P(), P()),
        check_vma=False)
```

profile of v0, /device:TPU:0, one launch (start us, length us, event | category | flops | bytes accessed | tf_op | source)
XLA Modules:
  0.0 496.3 jit_solution(9051066435268229546)
XLA Ops:
  7.2 0.0 all-gather.11.cloned.1.call-start
  7.2 0.7 all-gather.11.cloned.1.call-update
  7.9 0.0 all-gather.9.cloned.1.call-start
  7.9 0.7 all-gather.9.cloned.1.call-update
  8.6 0.0 all-gather.7.cloned.1.call-start
  8.7 0.7 all-gather.7.cloned.1.call-update
  9.4 0.0 all-gather.13.cloned.1.call-start
  9.4 0.5 all-gather.13.cloned.1.call-update
  10.0 0.0 all-gather.15.cloned.1.call-start
  10.0 0.5 all-gather.15.cloned.1.call-update
  10.5 0.0 all-gather.17.cloned.1.call-start
  10.6 0.5 all-gather.17.cloned.1.call-update
  11.1 0.0 reduce-scatter.2.cloned.1.call-start
  11.2 23.4 %copy.19 = bf16[1,3,960,2560]{2,3,1,0:T(8,128)(2,1)} copy(f32[1,3,960,2560]{3,2,1,0:T(8,128)} %param.17) | data formatting | bytes 44236800 | tf_op args[8]
  34.6 0.0 reduce-scatter.2.cloned.1.call-update
  34.6 15.0 %all-gather.11.cloned.1.call-done = bf16[960,2560]{0,1:T(8,128)(2,1)} async-done(((bf16[960,320]{0,1:T(8,128)(2,1)}), bf16[960,2560]{0,1:T(8,128)(2,1)}) %all-gather.11.cloned.1.call-update) | async-done | bytes 4915216 | tf_op jit(solution)/shard_map/all_gather | solution.py:31
  49.6 29.7 %fusion.6 = f32[4096,2560]{1,0:T(8,128)} fusion(bf16[4096,960]{0,1:T(8,128)(2,1)} %param.9, bf16[960,2560]{0,1:T(8,128)(2,1)} %all-gather.11.cloned.1.call-done), kind=kOutput, calls=%fused_computation.14 | convolution fusion | flops 20132659200 | bytes 54722560 | tf_op jit(solution)/shard_map/dot_general | solution.py:11
  79.3 9.1 %all-gather.9.cloned.1.call-done = bf16[960,2560]{0,1:T(8,128)(2,1)} async-done(((bf16[960,320]{0,1:T(8,128)(2,1)}), bf16[960,2560]{0,1:T(8,128)(2,1)}) %all-gather.9.cloned.1.call-update) | async-done | bytes 4915216 | tf_op jit(solution)/shard_map/all_gather | solution.py:32
  88.4 29.8 %fusion.5 = f32[4096,2560]{1,0:T(8,128)} fusion(bf16[4096,960]{0,1:T(8,128)(2,1)} %param.9, bf16[960,2560]{0,1:T(8,128)(2,1)} %all-gather.9.cloned.1.call-done), kind=kOutput, calls=%fused_computation.13 | convolution fusion | flops 20132659200 | bytes 54722560 | tf_op jit(solution)/shard_map/dot_general | solution.py:12
  118.3 9.0 %all-gather.7.cloned.1.call-done = bf16[2560,960]{1,0:T(8,128)(2,1)} async-done(((bf16[320,960]{1,0:T(8,128)(2,1)}), bf16[2560,960]{1,0:T(8,128)(2,1)}) %all-gather.7.cloned.1.call-update) | async-done | bytes 4915216 | tf_op jit(solution)/shard_map/all_gather | solution.py:33
  127.3 56.2 %multiply_convert_fusion.1 = (bf16[4096,2560]{1,0:T(8,128)(2,1)}, bf16[4096,2560]{1,0:T(8,128)(2,1)}) fusion(f32[4096,2560]{1,0:T(8,128)} %fusion.6, f32[4096,2560]{1,0:T(8,128)} %fusion.5, bf16[4096,960]{0,1:T(8,128)(2,1)} %param.10, bf16[2560,960]{1,0:T(8,128)(2,1)} %all-gather.7.cloned.1.call-done), kind=kOutput, calls=%fused_computation.1 | convolution fusion | flops 20268974080 | bytes 138608640 | tf_op jit(solution)/shard_map/td,fd->tf/dot_general | solution.py:16
  183.5 27.0 %convolution_bitcast_fusion = f32[1,960,2560]{2,1,0:T(8,128)} fusion(bf16[4096,960]{0,1:T(8,128)(2,1)} %param.9, bf16[4096,2560]{1,0:T(8,128)(2,1)} %get-tuple-element.12), kind=kOutput, calls=%fused_computation.9 | convolution fusion | flops 20132659200 | bytes 38666240 | tf_op jit(solution)/shard_map/td,tf->df/dot_general | solution.py:23
  210.4 0.0 all-gather.13.cloned.1.call-done
  210.4 7.9 %copy.20 = bf16[960,2560]{1,0:T(8,128)(2,1)} copy(bf16[960,2560]{0,1:T(8,128)(2,1)} %all-gather.13.cloned.1.call-done) | data formatting | bytes 9830400
  218.3 0.0 all-gather.15.cloned.1.call-done
  218.3 7.9 %copy.21 = bf16[960,2560]{1,0:T(8,128)(2,1)} copy(bf16[960,2560]{0,1:T(8,128)(2,1)} %all-gather.15.cloned.1.call-done) | data formatting | bytes 9830400
  226.2 17.1 %all-gather.17.cloned.1.call-done = bf16[2560,960]{1,0:T(8,128)(2,1)} async-done(((bf16[320,960]{1,0:T(8,128)(2,1)}), bf16[2560,960]{1,0:T(8,128)(2,1)}) %all-gather.17.cloned.1.call-update) | async-done | bytes 4915216 | tf_op jit(solution)/shard_map/all_gather | solution.py:36
  243.3 7.9 %copy.22 = bf16[2560,960]{0,1:T(8,128)(2,1)} copy(bf16[2560,960]{1,0:T(8,128)(2,1)} %all-gather.17.cloned.1.call-done) | data formatting | bytes 9830400
  251.2 26.9 %convolution_bitcast_fusion.1 = f32[1,960,2560]{2,1,0:T(8,128)} fusion(bf16[4096,960]{0,1:T(8,128)(2,1)} %param.9, bf16[4096,2560]{1,0:T(8,128)(2,1)} %get-tuple-element.13), kind=kOutput, calls=%fused_computation.10 | convolution fusion | flops 20132659200 | bytes 38666240 | tf_op jit(solution)/shard_map/td,tf->df/dot_general | solution.py:22
  278.1 39.1 %fusion.3 = f32[1,960,2560]{2,1,0:T(8,128)} fusion(bf16[4096,960]{0,1:T(8,128)(2,1)} %param.10, f32[4096,2560]{1,0:T(8,128)} %fusion.5, f32[4096,2560]{1,0:T(8,128)} %fusion.6), kind=kOutput, calls=%fused_computation.11 | convolution fusion | flops 20195573760 | bytes 101580800 | tf_op jit(solution)/shard_map/td,tf->df/dot_general | solution.py:24
  317.2 20.9 %maximum_bitcast_fusion = f32[1,3,960,2560]{3,2,1,0:T(8,128)} fusion(f32[1,960,2560]{2,1,0:T(8,128)} %fusion.3, f32[1,960,2560]{2,1,0:T(8,128)} %convolution_bitcast_fusion, f32[1,960,2560]{2,1,0:T(8,128)} %convolution_bitcast_fusion.1), kind=kLoop, calls=%fused_computation.5 | loop fusion | flops 14745600 | bytes 58982400 | tf_op jit(solution)/shard_map/broadcast_in_dim | solution.py:40
  338.0 27.4 %fusion.7 = f32[4096,960]{0,1:T(8,128)} fusion(bf16[4096,2560]{1,0:T(8,128)(2,1)} %get-tuple-element.13, bf16[960,2560]{0,1:T(8,128)(2,1)} %all-gather.11.cloned.1.call-done), kind=kOutput, calls=%fused_computation.15 | convolution fusion | flops 20132659200 | bytes 41615360 | tf_op jit(solution)/shard_map/tf,df->td/dot_general | solution.py:19
  365.4 28.0 %add_convert_fusion = bf16[4096,960]{0,1:T(8,128)(2,1)} fusion(f32[4096,960]{0,1:T(8,128)} %fusion.7, bf16[4096,2560]{1,0:T(8,128)(2,1)} %get-tuple-element.12, bf16[960,2560]{0,1:T(8,128)(2,1)} %all-gather.9.cloned.1.call-done), kind=kOutput, calls=%fused_computation.8 | convolution fusion | flops 20140523520 | bytes 49479680 | tf_op jit(solution)/shard_map/tf,df->td/dot_general | solution.py:20
  393.4 0.0 reduce-scatter.2.cloned.1.call-done
  393.4 95.6 %all-reduce.1 = f32[3,960,320]{1,2,0:T(8,128)} all-reduce(bf16[3,960,320]{1,2,0:T(8,128)(2,1)} %reduce-scatter.2.cloned.1.call-done), channel_id=1, replica_groups=mesh['dp'=2,'col'=2,'fsdp'=4] {'dp'}, use_global_device_ids=true, to_apply=%region_1.0 | all-reduce | flops 921600 | bytes 5529600 | tf_op jit(solution)/shard_map/psum | solution.py:38
Async XLA Ops:
  7.2 42.5 %all-gather.11.cloned.1.call-start = ((), (), s32[]{:S(2)}) async-start(), calls=%async_computation.3 | async-start | bytes 5898240 | tf_op jit(solution)/shard_map/all_gather | solution.py:31
  7.9 80.5 %all-gather.9.cloned.1.call-start = ((), (), s32[]{:S(2)}) async-start(), calls=%async_computation.2 | async-start | bytes 5898240 | tf_op jit(solution)/shard_map/all_gather | solution.py:32
  8.6 118.6 %all-gather.7.cloned.1.call-start = ((), (), s32[]{:S(2)}) async-start(), calls=%async_computation.1 | async-start | bytes 5898240 | tf_op jit(solution)/shard_map/all_gather | solution.py:33
  9.4 201.1 %all-gather.13.cloned.1.call-start = ((), (), s32[]{:S(2)}) async-start(), calls=%async_computation.5 | async-start | bytes 5898240 | tf_op jit(solution)/shard_map/all_gather | solution.py:34
  10.0 208.4 %all-gather.15.cloned.1.call-start = ((), (), s32[]{:S(2)}) async-start(), calls=%async_computation.6 | async-start | bytes 5898240 | tf_op jit(solution)/shard_map/all_gather | solution.py:35
  10.5 232.8 %all-gather.17.cloned.1.call-start = ((), (), s32[]{:S(2)}) async-start(), calls=%async_computation.7 | async-start | bytes 5898240 | tf_op jit(solution)/shard_map/all_gather | solution.py:36
  11.1 382.3 %reduce-scatter.2.cloned.1.call-start = ((), (), s32[]{:S(2)}) async-start(), calls=%async_computation.4 | async-start | bytes 17694720 | tf_op jit(solution)/shard_map/reduce_scatter | solution.py:37
Sparse Core Ops, SparseCore 0:
  9.8 39.7 all-gather.10
  51.5 36.9 all-gather.8
  90.3 36.9 all-gather.6
  129.0 36.9 all-gather.12
  167.6 36.9 all-gather.14
  206.3 36.9 all-gather.16
  246.8 100.2 reduce-scatter.1
where the time goes:
time: 505 us; the launch traced here: 496 us
  matrix products  264 us (52%)
  blocking collectives  95.6 us (19%)
  waiting for transfers between devices  53.9 us (11%)
  local copies, waits for them, and re-layouts  47.1 us (9%)
  other arithmetic  20.9 us (4%)
  between operations  14.6 us (3%)
    psum x1, blocking collectives, device_step(): grad_next = lax.psum(grad_shard.astype(jnp.float32), 'dp')  95.6 us
    dot_general x1, matrix products, local_backward(): jnp.einsum('td,fd->tf', dy_loc, down_full, preferred_element_type=jnp.flo...  56.2 us
    unnamed x4, local copies, waits for them, and re-layouts  47.1 us
    dot_general x1, matrix products, local_backward(): jnp.einsum('td,tf->df', dy_loc, hidden, preferred_element_type=jnp.float32)  39.1 us
    dot_general x1, matrix products, local_backward(): pre_up = jnp.dot(x_loc, up_full, preferred_element_type=jnp.float32)  29.8 us
    dot_general x1, matrix products, local_backward(): pre_gate = jnp.dot(x_loc, gate_full, preferred_element_type=jnp.float32)  29.7 us
    dot_general x1, matrix products, local_backward(): jnp.einsum('tf,df->td', d_up, up_full, preferred_element_type=jnp.float32)  28 us
    dot_general x1, matrix products, local_backward(): jnp.einsum('tf,df->td', d_gate, gate_full, preferred_element_type=jnp.flo...  27.4 us
  transfers between devices with their start and end apart: 7, of which 4 were waited for; matrix products, arithmetic and copies ran while one was open for 67% of the time, Pallas kernels for 0%

commit v1 on v0

v1 whole, which is shorter than its diff:
```python
import jax
import jax.numpy as jnp
from jax import lax
from jax.experimental import pallas as pl
from jax.experimental.pallas import tpu as pltpu
from jax.sharding import PartitionSpec as P

ALL_AXES = ('dp', 'col', 'fsdp')
FSDP_AXES = ('col', 'fsdp')
MESH = pl.DeviceIdType.MESH
BF16 = jnp.bfloat16
F32 = jnp.float32

D = 960
F = 2560
T = 4096
SH = F // 8
CH = F // 4
TM = 512
NI = T // TM
NC = 4
SUB = 320

NN = (((1,), (0,)), ((), ()))
NT = (((1,), (1,)), ((), ()))


def dotf(a, b, dims):
    return lax.dot_general(a, b, dims, preferred_element_type=F32)


def step_kernel(x_hbm, dy_hbm, w1_hbm, w3_hbm, w2_hbm, v1_hbm, v3_hbm, v2_hbm,
                h3_hbm, dx_hbm, v_out,
                x_v, dy_v, acc, w_v, wt, hbuf,
                lsem, hsem, xsem, send, recv):
    z = lax.axis_index('dp')
    y = lax.axis_index('col')
    fs = lax.axis_index('fsdp')
    x = fs // 2
    c = fs % 2
    partner = {'fsdp': x * 2 + (1 - c)}
    xnbr = {'fsdp': (1 - x) * 2 + c}
    ynbr = {'col': 1 - y}
    znbr = {'dp': 1 - z}
    q_own = y * 2 + x
    q_x = y * 2 + (1 - x)
    q_y = (1 - y) * 2 + x
    q_d = (1 - y) * 2 + (1 - x)

    def remote(src, dst, dev, k):
        return pltpu.make_async_remote_copy(src, dst, send.at[k], recv.at[k],
                                            device_id=dev, device_id_type=MESH)

    class Gather:
        def __init__(self, base, srcs, dst, zsplit):
            self.base, self.srcs, self.dst, self.zsplit = base, srcs, dst, zsplit
            self.lo = z * 160 if zsplit else 0
            self.n = 160 if zsplit else 320

        def blk(self, a, q, lo, n):
            return self.dst.at[a, pl.ds(pl.multiple_of(q * CH + c * SH + lo, 16), n), :]

        def copy(self, kind, a):
            k = self.base + 3 * ('x0', 'x1', 'y0', 'y1', 'xf', 'yf', 'zx', 'zy', 'zd', 'dx', 'dy', 'dd').index(kind) + a
            h = self.n // 2
            if kind in ('x0', 'x1', 'y0', 'y1'):
                lo = self.lo + (h if kind[1] == '1' else 0)
                return remote(self.srcs[a].at[pl.ds(pl.multiple_of(lo, 16), h), :], self.blk(a, q_own, lo, h),
                              xnbr if kind[0] == 'x' else ynbr, k)
            if kind == 'yf':
                return remote(self.blk(a, q_x, self.lo, h), self.blk(a, q_x, self.lo, h), ynbr, k)
            if kind == 'xf':
                return remote(self.blk(a, q_y, self.lo + h, h), self.blk(a, q_y, self.lo + h, h), xnbr, k)
            q = {'x': q_x, 'y': q_y, 'd': q_d}[kind[1]]
            if kind[0] == 'z':
                return remote(self.blk(a, q, self.lo, self.n), self.blk(a, q, self.lo, self.n), znbr, k)
            return remote(self.blk(a, q, 0, SH), self.blk(a, q, 0, SH), partner, k)

        def start(self, *kinds):
            for kind in kinds:
                for a in range(3):
                    self.copy(kind, a).start()

        def recv(self, *kinds):
            for kind in kinds:
                for a in range(3):
                    self.copy(kind, a).wait_recv()

        def sent(self):
            for kind in ('x0', 'x1', 'y0', 'y1', 'xf', 'yf', 'dx', 'dy', 'dd') + (
                    ('zx', 'zy', 'zd') if self.zsplit else ()):
                for a in range(3):
                    self.copy(kind, a).wait_send()

    w_hbm = (w1_hbm, w3_hbm, w2_hbm)
    v_hbm = (v1_hbm, v3_hbm, v2_hbm)
    gw = Gather(0, w_hbm, w_v, True)
    gv = Gather(36, v_hbm, v_out, False)

    def local(src, dst, k):
        return pltpu.make_async_copy(src, dst, lsem.at[k])

    pw = [remote(w_hbm[a], gw.blk(a, q_own, 0, SH), partner, 72 + a) for a in range(3)]
    pv = [remote(v_hbm[a], gv.blk(a, q_own, 0, SH), partner, 75 + a) for a in range(3)]
    lw = [local(w_hbm[a], gw.blk(a, q_own, 0, SH), a) for a in range(3)]
    lv = [local(v_hbm[a], gv.blk(a, q_own, 0, SH), 3 + a) for a in range(3)]
    lx = [local(x_hbm, x_v, 6), local(dy_hbm, dy_v, 7)]

    for cp in lw + lx:
        cp.start()
    bar = pltpu.get_barrier_semaphore()
    for dev in (partner, xnbr, ynbr, znbr):
        pl.semaphore_signal(bar, inc=1, device_id=dev, device_id_type=MESH)
    pl.semaphore_wait(bar, 4)
    for cp in pw:
        cp.start()
    gw.start('x0', 'y1', 'x1', 'y0')

    def zero(r, _):
        acc[pl.ds(pl.multiple_of(r * 16, 16), 16), :] = jnp.zeros((16, T), F32)
        return 0
    lax.fori_loop(0, D // 16, zero, 0)

    for cp in lw + lx:
        cp.wait()
    for cp in pw:
        cp.wait_recv()

    def body(n, _):
        j = n // NI
        i = n % NI

        def at(k):
            return pl.when(n == k)

        @at(3)
        def _():
            gw.recv('x0', 'x1')
            gw.start('zx', 'yf')
            gw.recv('y0', 'y1')
            gw.start('xf', 'zy')

        @at(8)
        def _():
            gw.recv('zx')
            gw.start('dx')
            gw.recv('dx')

        @at(10)
        def _():
            for cp in lv + pv:
                cp.start()
            gv.start('x0', 'y1', 'x1', 'y0')
            gw.recv('xf', 'yf')
            gw.start('zd')

        @at(14)
        def _():
            gw.recv('zy')
            gw.start('dy')

        @at(16)
        def _():
            gw.recv('dy')

        @at(20)
        def _():
            gw.recv('zd')
            gw.start('dd')

        @at(22)
        def _():
            gv.recv('x0')
            gv.start('yf')
            gv.recv('y1')
            gv.start('xf')

        @at(24)
        def _():
            gw.recv('dd')

        @at(26)
        def _():
            gv.recv('x1', 'y0')
            gv.start('dx', 'dy')

        q = jnp.where(j == 0, q_own, jnp.where(j == 1, q_x, jnp.where(j == 2, q_y, q_d)))
        base = pl.multiple_of(q * CH, CH)

        @pl.when(i == 0)
        def _():
            def tr(r, _):
                src = pl.ds(pl.multiple_of(base + r * 128, 128), 128)
                for a in range(2):
                    wt[:, pl.ds(pl.multiple_of(a * CH + r * 128, 128), 128)] = w_v[a, src, :].T
                return 0
            lax.fori_loop(0, CH // 128, tr, 0)

        cols = pl.ds(pl.multiple_of(i * TM, TM), TM)
        slot = n % 2

        def hcopies(slot):
            return [pltpu.make_async_copy(hbuf.at[slot, pl.ds(a * CH, CH), :],
                                          h3_hbm.at[a, pl.ds(base, CH), cols], hsem.at[slot, a]) for a in range(3)]

        @pl.when(n >= 2)
        def _():
            for cp in hcopies(slot):
                cp.wait()

        for r in range(CH // SUB):
            src = pl.ds(pl.multiple_of(base + r * SUB, 16), SUB)
            a = dotf(w_v[0, src, :], x_v[:, cols], NN)
            b = dotf(w_v[1, src, :], x_v[:, cols], NN)
            dh = dotf(w_v[2, src, :], dy_v[:, cols], NN)
            s = 1.0 / (1.0 + jnp.exp(-a))
            act = a * s
            hbuf[slot, r * SUB:(r + 1) * SUB, :] = (dh * b * s * (1.0 + a * (1.0 - s))).astype(BF16)
            hbuf[slot, CH + r * SUB:CH + (r + 1) * SUB, :] = (dh * act).astype(BF16)
            hbuf[slot, 2 * CH + r * SUB:2 * CH + (r + 1) * SUB, :] = (act * b).astype(BF16)
        for cp in hcopies(slot):
            cp.start()
        acc[:, cols] += dotf(wt[...], hbuf[slot, 0:2 * CH, :], NN)

        @pl.when(j == NC - 1)
        def _():
            x_v[:, cols] = acc[:, cols].astype(BF16)
            pltpu.make_async_copy(x_v.at[:, cols], dx_hbm.at[:, cols], xsem).start()
        return 0

    lax.fori_loop(0, NC * NI, body, 0)

    gv.recv('xf', 'yf')
    gv.start('dd')
    for slot in range(2):
        for a in range(3):
            pltpu.make_async_copy(hbuf.at[slot, pl.ds(a * CH, CH), :],
                                  h3_hbm.at[a, pl.ds(0, CH), pl.ds(0, TM)], hsem.at[slot, a]).wait()
    pltpu.make_async_copy(x_v, dx_hbm, xsem).wait()
    for cp in lv:
        cp.wait()
    for cp in pv:
        cp.wait_recv()
    gv.recv('dx', 'dy', 'dd')
    for cp in pw + pv:
        cp.wait_send()
    gw.sent()
    gv.sent()


def run_step(*args):
    hbm = pl.BlockSpec(memory_space=pltpu.MemorySpace.HBM)
    return pl.pallas_call(
        step_kernel,
        out_shape=(jax.ShapeDtypeStruct((3, F, T), BF16), jax.ShapeDtypeStruct((D, T), BF16),
                   jax.ShapeDtypeStruct((3, F, D), BF16)),
        in_specs=[hbm] * 8,
        out_specs=(hbm,) * 3,
        scratch_shapes=[
            pltpu.VMEM((D, T), BF16), pltpu.VMEM((D, T), BF16), pltpu.VMEM((D, T), F32),
            pltpu.VMEM((3, F, D), BF16), pltpu.VMEM((D, 2 * CH), BF16),
            pltpu.VMEM((2, 3 * CH, TM), BF16),
            pltpu.SemaphoreType.DMA((8,)), pltpu.SemaphoreType.DMA((2, 3)), pltpu.SemaphoreType.DMA,
            pltpu.SemaphoreType.DMA((78,)), pltpu.SemaphoreType.DMA((78,)),
        ],
        compiler_params=pltpu.CompilerParams(collective_id=0, has_side_effects=True,
                                             vmem_limit_bytes=66_000_000),
        cost_estimate=pl.CostEstimate(flops=10 * T * D * F, bytes_accessed=120_000_000, transcendentals=T * F),
    )(*args)


def grad_kernel(x_ref, dy_ref, h3_ref, dx_ref, v_ref,
                dw_ref, dxo_ref, v1o_ref, v3o_ref, v2o_ref):
    s = pl.program_id(0)
    for k, (lhs, vo) in enumerate(((x_ref, v1o_ref), (x_ref, v3o_ref), (dy_ref, v2o_ref))):
        @pl.when(s // 5 == k)
        def _():
            dxo_ref[...] = dx_ref[...]
            vo[...] = v_ref[0].T
            dw_ref[0, 0] = dotf(lhs[...], h3_ref[0], NT)


def run_grad(x, dy, h3, dx, v):
    one = pl.Buffered(1)
    whole = pl.BlockSpec((D, T), lambda s: (0, 0), pipeline_mode=one)
    dxs = pl.BlockSpec((D // 15, T), lambda s: (s, 0))

    def vspec(k):
        return pl.BlockSpec((D, 512), lambda s: (0, jnp.clip(s - 5 * k, 0, 4)))
    return pl.pallas_call(
        grad_kernel,
        grid=(15,),
        out_shape=(jax.ShapeDtypeStruct((1, 3, D, F), F32), jax.ShapeDtypeStruct((D, T), BF16),
                   jax.ShapeDtypeStruct((D, F), BF16), jax.ShapeDtypeStruct((D, F), BF16),
                   jax.ShapeDtypeStruct((D, F), BF16)),
        in_specs=[whole, whole, pl.BlockSpec((1, 512, T), lambda s: (s // 5, s % 5, 0)), dxs,
                  pl.BlockSpec((1, 512, D), lambda s: (s // 5, s % 5, 0))],
        out_specs=(pl.BlockSpec((1, 1, D, 512), lambda s: (0, s // 5, 0, s % 5)), dxs, vspec(0), vspec(1), vspec(2)),
        compiler_params=pltpu.CompilerParams(vmem_limit_bytes=64_000_000),
        cost_estimate=pl.CostEstimate(flops=6 * T * D * F, bytes_accessed=150_000_000, transcendentals=0),
    )(x, dy, h3, dx, v)


def solution(mesh):
    def device_step(x, dy, w1, w3, w2, v1, v3, v2, g_next):
        part = lax.psum_scatter(g_next[0].astype(BF16), FSDP_AXES, scatter_dimension=2, tiled=True)
        xt, dyt = x.T, dy.T
        h3, dx, v = run_step(xt, dyt, w1.T, w3.T, w2, v1.T, v3.T, v2)
        other = lax.ppermute(part, 'dp', [(0, 1), (1, 0)])
        dw, dxo, v1o, v3o, v2o = run_grad(xt, dyt, h3, dx, v)
        grad_next = part.astype(F32) + other.astype(F32)
        return dxo.T, grad_next, dw, v1o, v3o, v2o.T

    row_spec = P(ALL_AXES, None)
    col_shard = P(None, FSDP_AXES)
    row_shard = P(FSDP_AXES, None)
    dev_spec = P(ALL_AXES, None, None, None)
    return jax.shard_map(
        device_step, mesh=mesh,
        in_specs=(row_spec, row_spec, col_shard, col_shard, row_shard, col_shard, col_shard, row_shard, dev_spec),
        out_specs=(row_spec, P(None, None, FSDP_AXES), dev_spec, P(), P(), P()),
        check_vma=False)
```

time: 505 us -> 291 us (0.58); the launches traced: 496 us -> 291 us
  matrix products: 264 us -> 0 us
  Pallas kernels: 0 us -> 248 us
  blocking collectives: 95.6 us -> 0 us
  waiting for transfers between devices: 53.9 us -> 0.04 us
  local copies, waits for them, and re-layouts: 47.1 us -> 23.4 us
  other arithmetic: 20.9 us -> 4.3 us
    dot_general x8 -> x0, matrix products: 264 us -> none  [the longest x1 56.2 us: local_backward(): jnp.einsum('td,fd->tf', dy_loc, down_full, preferred_element_type=jnp.flo...]
    pallas_call x0 -> x2, Pallas kernels: none -> 248 us  [the longest x1 171 us: run_step(): pl.pallas_call(step_kernel, out_shape=(jax.ShapeDtypeStruct((3, F, T), BF...]
    psum x1 -> x0, blocking collectives: 95.6 us -> none  [device_step(): grad_next = lax.psum(grad_shard.astype(jnp.float32), 'dp')]
    all_gather x6 -> x0, waiting for transfers between devices: 50.2 us -> none  [the longest x1 17.1 us: device_step(): v_down_full = lax.all_gather(v_down, FSDP_AXES, axis=0, tiled=True)]
    unnamed x4 -> x3, local copies, waits for them, and re-layouts: 47.1 us -> 23.4 us
    broadcast_in_dim x1 -> x0, other arithmetic: 20.9 us -> none  [device_step(): grad_local[None]]
  transfers between devices with their start and end apart: 7 -> 2, of which waited for: 4 -> 0; matrix products, arithmetic and copies ran while one was open for 67% -> 0% of each run, Pallas kernels for 0% -> 85%
where the time goes in v1:
time: 291 us
  Pallas kernels  248 us (85%)
  local copies, waits for them, and re-layouts  23.4 us (8%)
  between operations  14.1 us (5%)
  other arithmetic  4.3 us (1%)
    pallas_call x1, Pallas kernels, run_step(): pl.pallas_call(step_kernel, out_shape=(jax.ShapeDtypeStruct((3, F, T), BF...  171 us
    pallas_call x1, Pallas kernels, run_grad(): pl.pallas_call(grad_kernel, grid=(15,), out_shape=(jax.ShapeDtypeStruct((...  76.4 us
    unnamed x3, local copies, waits for them, and re-layouts  23.4 us
  transfers between devices with their start and end apart: 2, of which 0 were waited for; matrix products, arithmetic and copies ran while one was open for 0% of the time, Pallas kernels for 85%

profile of v1, /device:TPU:0, one launch (start us, length us, event | category | flops | bytes accessed | tf_op | source)
XLA Modules:
  0.0 290.7 jit_solution(2119181104280979267)
XLA Ops:
  7.2 0.0 reduce-scatter.2.cloned.1.call-start
  7.2 23.4 %copy.15 = bf16[1,3,960,2560]{2,3,1,0:T(8,128)(2,1)} copy(f32[1,3,960,2560]{3,2,1,0:T(8,128)} %param.17) | data formatting | bytes 44236800 | tf_op args[8]
  30.6 0.0 reduce-scatter.2.cloned.1.call-update
  30.6 171.2 %shard_map.136 = (bf16[3,2560,4096]{2,1,0:T(8,128)(2,1)}, bf16[960,4096]{1,0:T(8,128)(2,1)}, bf16[3,2560,960]{2,1,0:T(8,128)(2,1)}) custom-call(bf16[960,4096]{1,0:T(8,128)(2,1)} %bitcast.12, bf16[960,4096]{1,0:T(8,128)(2,1)} %bitcast.14, bf16[320,960]{1,0:T(8,128)(2,1)} %bitcast.16, bf16[320,960]{1,0:T(8,128)(2,1)} %bitcast.17, bf16[320,960]{1,0:T(8,128)(2,1)} %w2_hbm.1, ...), custom_call_target="tpu_custom_call" | custom-call | flops 100663296000 | bytes 120000000 | tf_op jit(solution)/shard_map/pallas_call | solution.py:253
  201.8 0.0 reduce-scatter.2.cloned.1.call-done
  201.8 1.3 collective-permute-start
  203.1 0.0 copy-start
  203.1 76.4 %shard_map.137 = (f32[1,3,960,2560]{3,2,1,0:T(8,128)}, bf16[960,4096]{1,0:T(8,128)(2,1)}, bf16[960,2560]{1,0:T(8,128)(2,1)}, bf16[960,2560]{1,0:T(8,128)(2,1)}, bf16[960,2560]{1,0:T(8,128)(2,1)}) custom-call(bf16[960,4096]{1,0:T(8,128)(2,1)} %bitcast.13, bf16[960,4096]{1,0:T(8,128)(2,1)} %bitcast.15, bf16[3,2560,4096]{2,1,0:T(8,128)(2,1)} %get-tuple-element.14.h3_ref, ...), custom_call_target="tpu_custom_call" | custom-call | flops 60397977600 | bytes 150000000 | tf_op jit(solution)/shard_map/pallas_call | solution.py:290
  279.5 0.0 collective-permute-done
  279.5 0.0 copy-done
  279.6 4.3 %convert_add_fusion = f32[3,960,320]{1,2,0:T(8,128)} fusion(bf16[3,960,320]{1,2,0:T(8,128)(2,1)} %collective-permute-done, bf16[3,960,320]{1,2,0:T(8,128)(2,1)S(1)} %copy-done), kind=kLoop, calls=%fused_computation.1 | loop fusion | flops 2764800 | bytes 7372800 | tf_op jit(solution)/shard_map/add | solution.py:311
Async XLA Ops:
  7.2 194.7 %reduce-scatter.2.cloned.1.call-start = ((), (), s32[]{:S(2)}) async-start(), calls=%async_computation.1 | async-start | bytes 17694720 | tf_op jit(solution)/shard_map/reduce_scatter | solution.py:306
  201.8 77.7 %collective-permute-start = (bf16[3,960,320]{1,2,0:T(8,128)(2,1)}, bf16[3,960,320]{1,2,0:T(8,128)(2,1)}, u32[]{:S(2)}, u32[]{:S(2)}) collective-permute-start(bf16[3,960,320]{1,2,0:T(8,128)(2,1)} %reduce-scatter.2.cloned.1.call-done), channel_id=1, source_target_pairs={{0,8},{8,0},{1,9},{9,1},{2,10},{10,2},{3,11},{11,3},{4,12},{12,4},... | collective-permute-start | bytes 5529608 | tf_op jit(solution)/shard_map/ppermute | solution.py:309
  203.1 76.4 %copy-start = (bf16[3,960,320]{1,2,0:T(8,128)(2,1)S(1)}, bf16[3,960,320]{1,2,0:T(8,128)(2,1)}, u32[]{:S(2)}) copy-start(bf16[3,960,320]{1,2,0:T(8,128)(2,1)} %reduce-scatter.2.cloned.1.call-done) | copy-start | bytes 5529604
Sparse Core Ops, SparseCore 0:
  30.8 149.6 reduce-scatter.1

commit v2 on v1

v2 whole, which is shorter than its diff:
```python
import jax
import jax.numpy as jnp
from jax import lax
from jax.experimental import pallas as pl
from jax.experimental.pallas import tpu as pltpu
from jax.sharding import PartitionSpec as P

ALL_AXES = ('dp', 'col', 'fsdp')
FSDP_AXES = ('col', 'fsdp')
MESH = pl.DeviceIdType.MESH
BF16 = jnp.bfloat16
F32 = jnp.float32

D = 960
F = 2560
T = 4096
SH = F // 8
CH = F // 4
TM = 512
NI = T // TM
NC = 4
SUB = 320
HR = D // 2
QR = HR // 2
S2 = 3
G_AT = (13, 16, 18, 20, 23, 25)

NN = (((1,), (0,)), ((), ()))
NT = (((1,), (1,)), ((), ()))


def dotf(a, b, dims):
    return lax.dot_general(a, b, dims, preferred_element_type=F32)


def step_kernel(x_hbm, dy_hbm, w1_hbm, w3_hbm, w2_hbm, v1_hbm, v3_hbm, v2_hbm, g_hbm,
                h3_hbm, dx_hbm, v_out, sg, r1, pp, rx, ry, rx2, ry2, sx, sy,
                x_v, dy_v, acc, w_v, wt, hbuf, gin1, gout1, gin2, rin, gout2, ab, ob,
                lsem, hsem, xsem, send, recv, g1l, g1s, g1r, g2l, gps, gpr, abl, obs, gms, gmr, zs, zr):
    z = lax.axis_index('dp')
    y = lax.axis_index('col')
    fs = lax.axis_index('fsdp')
    x = fs // 2
    c = fs % 2
    partner = {'fsdp': x * 2 + (1 - c)}
    xnbr = {'fsdp': (1 - x) * 2 + c}
    ynbr = {'col': 1 - y}
    znbr = {'dp': 1 - z}
    q_own = y * 2 + x
    q_x = y * 2 + (1 - x)
    q_y = (1 - y) * 2 + x
    q_d = (1 - y) * 2 + (1 - x)

    def rdma(src, dst, ssem, rsem, dev):
        return pltpu.make_async_remote_copy(src, dst, ssem, rsem, device_id=dev, device_id_type=MESH)

    def remote(src, dst, dev, k):
        return rdma(src, dst, send.at[k], recv.at[k], dev)

    class Gather:
        KINDS = ('x0', 'x1', 'y0', 'y1', 'xf', 'yf', 'dx', 'dy', 'dd', 'zx0', 'zx1', 'zy0', 'zy1', 'zd0', 'zd1')

        def __init__(self, base, srcs, dst, arrays, zsplit):
            self.base, self.srcs, self.dst, self.arrays, self.zsplit = base, srcs, dst, arrays, zsplit
            self.lo = z * 160 if zsplit else 0
            self.n = 160 if zsplit else 320

        def blk(self, a, q, lo, n):
            return self.dst.at[a, pl.ds(pl.multiple_of(q * CH + c * SH + lo, 16), n), :]

        def copy(self, kind, a):
            k = self.base + len(self.arrays) * self.KINDS.index(kind) + self.arrays.index(a)
            h = self.n // 2
            if kind in ('x0', 'x1', 'y0', 'y1'):
                lo = self.lo + h * int(kind[1])
                return remote(self.srcs[a].at[pl.ds(pl.multiple_of(lo, 16), h), :], self.blk(a, q_own, lo, h),
                              xnbr if kind[0] == 'x' else ynbr, k)
            if kind == 'yf':
                return remote(self.blk(a, q_x, self.lo, h), self.blk(a, q_x, self.lo, h), ynbr, k)
            if kind == 'xf':
                return remote(self.blk(a, q_y, self.lo + h, h), self.blk(a, q_y, self.lo + h, h), xnbr, k)
            q = {'x': q_x, 'y': q_y, 'd': q_d}[kind[1]]
            if kind[0] == 'z':
                b = self.blk(a, q, self.lo + h * int(kind[2]), h)
                return remote(b, b, znbr, k)
            return remote(self.blk(a, q, 0, SH), self.blk(a, q, 0, SH), partner, k)

        def start(self, *kinds):
            for kind in kinds:
                for a in self.arrays:
                    self.copy(kind, a).start()

        def recv(self, *kinds):
            for kind in kinds:
                for a in self.arrays:
                    self.copy(kind, a).wait_recv()

        def sent(self):
            for kind in self.KINDS[:15 if self.zsplit else 9]:
                for a in self.arrays:
                    self.copy(kind, a).wait_send()

    w_hbm = (w1_hbm, w3_hbm, w2_hbm)
    v_hbm = (v1_hbm, v3_hbm, v2_hbm)
    gw = Gather(0, w_hbm, w_v, (0, 1, 2), True)
    gva = Gather(45, v_hbm, v_out, (0,), True)
    gvb = Gather(60, v_hbm, v_out, (1, 2), False)

    def local(src, dst, k):
        return pltpu.make_async_copy(src, dst, lsem.at[k])

    pw = [remote(w_hbm[a], gw.blk(a, q_own, 0, SH), partner, 78 + a) for a in range(3)]
    pv = [remote(v_hbm[a], gva.blk(a, q_own, 0, SH), partner, 81 + a) for a in range(3)]
    lw = [local(w_hbm[a], gw.blk(a, q_own, 0, SH), a) for a in range(3)]
    lv = [local(v_hbm[a], gva.blk(a, q_own, 0, SH), 3 + a) for a in range(3)]
    lx = [local(x_hbm, x_v, 6), local(dy_hbm, dy_v, 7)]

    def cols_of(q):
        return pl.ds(pl.multiple_of(q * CH, 128), CH)

    def unit(u):
        m = u % 4
        q = jnp.where(m == 0, q_d, jnp.where(m == 1, q_x, jnp.where(m == 2, q_y, q_own)))
        return u // 4, cols_of(q)

    def half(h):
        return pl.ds(pl.multiple_of(h * HR, 16), HR)

    def g1_load(u):
        k, cq = unit(u)
        return pltpu.make_async_copy(g_hbm.at[k, half(1 - c), cq], gin1, g1l)

    def g1_send(u):
        k, _ = unit(u)
        return rdma(gout1, r1.at[u], g1s, g1r.at[u], partner)

    def g2_loads(u):
        k, cq = unit(u)
        return (pltpu.make_async_copy(g_hbm.at[k, half(c), cq], gin2, g2l.at[0]),
                pltpu.make_async_copy(r1.at[u], rin, g2l.at[1]))

    def g2_out(u):
        return pltpu.make_async_copy(gout2, pp.at[u], g2l.at[2])

    def px(k, m):
        return rdma(pp.at[4 * k + m, pl.ds(0, QR), :], rx.at[k, m], gps.at[0, k, m], gpr.at[0, k, m], xnbr)

    def py(k, m):
        return rdma(pp.at[4 * k + 2 * m, pl.ds(QR, QR), :], ry.at[k, m], gps.at[1, k, m], gpr.at[1, k, m], ynbr)

    def g_stage1(u):
        @pl.when(u > 0)
        def _():
            g1_send(u - 1).wait_send()
        g1_load(u).wait()

        def cast(r, _):
            rows = pl.ds(pl.multiple_of(r * 48, 16), 48)
            gout1[rows, :] = gin1[rows, :].astype(BF16)
            return 0
        lax.fori_loop(0, HR // 48, cast, 0)
        g1_send(u).start()

        @pl.when(u < 11)
        def _():
            g1_load(u + 1).start()

    def g_sends(u):
        g2_out(u).wait()
        k = u // 4

        @pl.when(u % 4 == 0)
        def _():
            px(k, 0).start()
            py(k, 0).start()

        @pl.when(u % 4 == 1)
        def _():
            px(k, 1).start()

        @pl.when(u % 4 == 2)
        def _():
            py(k, 1).start()

    def g_stage2(u):
        for cp in g2_loads(u):
            cp.wait()

        def add(r, _):
            rows = pl.ds(pl.multiple_of(r * 48, 16), 48)
            gout2[rows, :] = (gin2[rows, :].astype(BF16).astype(F32) + rin[rows, :].astype(F32)).astype(BF16)
            return 0
        lax.fori_loop(0, HR // 48, add, 0)
        g2_out(u).start()

        @pl.when(u < 11)
        def _():
            g1_send(u + 1).wait_recv()
            for cp in g2_loads(u + 1):
                cp.start()

    def mid_sends(k):
        return (rdma(sy.at[k], ry2.at[k], gms.at[0, k], gmr.at[0, k], ynbr),
                rdma(sx.at[k], rx2.at[k], gms.at[1, k], gmr.at[1, k], xnbr))

    def ab_loads(k, fin):
        lo, hi = pl.ds(0, QR), pl.ds(QR, QR)
        if fin:
            srcs = (pp.at[4 * k + 3, lo, :], rx.at[k, 1], ry2.at[k], pp.at[4 * k + 3, hi, :], ry.at[k, 1], rx2.at[k])
        else:
            srcs = (pp.at[4 * k + 2, lo, :], rx.at[k, 0], pp.at[4 * k + 1, hi, :], ry.at[k, 0])
        return [pltpu.make_async_copy(s, ab.at[n], abl.at[n]) for n, s in enumerate(srcs)]

    def sg_half(s, k):
        return sg.at[s, k, half(c), :]

    def ob_outs(k, fin):
        if fin:
            dst = [sg.at[0, k, pl.ds(pl.multiple_of(c * HR + p * QR, 16), QR), :] for p in range(2)]
        else:
            dst = [sy.at[k], sx.at[k]]
        return [pltpu.make_async_copy(ob.at[p], dst[p], obs.at[p]) for p in range(2)]

    def z_sends(k):
        return (rdma(sg_half(0, k), sg_half(1, k), zs.at[0, k], zr.at[0, k], znbr),
                rdma(sg_half(0, k), sg_half(0, k), zs.at[1, k], zr.at[1, k], partner))

    def z_fwd(k):
        return rdma(sg_half(1, k), sg_half(1, k), zs.at[2, k], zr.at[2, k], partner)

    def g_load(k, fin):
        if fin:
            px(k, 1).wait_recv()
            py(k, 1).wait_recv()
            for cp in mid_sends(k):
                cp.wait_recv()
        else:
            px(k, 0).wait_recv()
            py(k, 0).wait_recv()
        for cp in ab_loads(k, fin):
            cp.start()

    def g_add(k, fin):
        for cp in ab_loads(k, fin):
            cp.wait()
        per = 3 if fin else 2

        def add(r, _):
            rows = pl.ds(pl.multiple_of(r * 48, 16), 48)
            for p in range(2):
                t = ab[per * p, rows, :].astype(F32)
                for e in range(1, per):
                    t = t + ab[per * p + e, rows, :].astype(F32)
                ob[p, rows, :] = t.astype(BF16)
            return 0
        lax.fori_loop(0, QR // 48, add, 0)
        for cp in ob_outs(k, fin):
            cp.start()

    def g_push(k, fin):
        for cp in ob_outs(k, fin):
            cp.wait()
        for cp in (z_sends(k) if fin else mid_sends(k)):
            cp.start()

    for cp in lw + lx:
        cp.start()
    g1_load(0).start()
    bar = pltpu.get_barrier_semaphore()
    for dev in (partner, xnbr, ynbr, znbr):
        pl.semaphore_signal(bar, inc=1, device_id=dev, device_id_type=MESH)
    pl.semaphore_wait(bar, 4)
    for cp in pw:
        cp.start()
    gw.start('x0', 'y1', 'x1', 'y0')

    def zero(r, _):
        acc[pl.ds(pl.multiple_of(r * 16, 16), 16), :] = jnp.zeros((16, T), F32)
        return 0
    lax.fori_loop(0, D // 16, zero, 0)

    for cp in lw + lx:
        cp.wait()
    for cp in pw:
        cp.wait_recv()

    def body(n, _):
        j = n // NI
        i = n % NI

        def at(k):
            return pl.when(n == k)

        @pl.when(n < 12)
        def _():
            g_stage1(n)

        @at(S2 - 1)
        def _():
            g1_send(0).wait_recv()
            for cp in g2_loads(0):
                cp.start()

        @pl.when((n > S2) & (n <= S2 + 12))
        def _():
            g_sends(n - S2 - 1)

        @pl.when((n >= S2) & (n < S2 + 12))
        def _():
            g_stage2(n - S2)

        @at(3)
        def _():
            gw.recv('x0')
            gw.start('zx0', 'yf')
            gw.recv('y1')
            gw.start('xf')

        @at(5)
        def _():
            gw.recv('x1')
            gw.start('zx1', 'zy1')
            gw.recv('y0')
            gw.start('zy0')
            for cp in lv + pv:
                cp.start()

        @at(8)
        def _():
            gw.recv('zx0', 'zx1')
            gw.start('dx')
            gw.recv('dx')

        @at(12)
        def _():
            g1_send(11).wait_send()
            gw.recv('xf', 'yf')
            gw.start('zd0', 'zd1')

        @at(15)
        def _():
            gw.recv('zy0', 'zy1')
            gw.start('dy')
            gvb.start('x0', 'y1')

        @at(16)
        def _():
            gw.recv('dy')

        @at(18)
        def _():
            gvb.start('x1', 'y0')

        @at(20)
        def _():
            gva.start('x0', 'y1', 'x1', 'y0')

        @at(22)
        def _():
            gw.recv('zd0', 'zd1')
            gw.start('dd')

        @at(24)
        def _():
            gw.recv('dd')
            gvb.recv('x0')
            gvb.start('yf')
            gvb.recv('y1')
            gvb.start('xf')

        @at(28)
        def _():
            gva.recv('x0')
            gva.start('yf', 'zx0')
            gva.recv('y1')
            gva.start('xf', 'zy1')
            gvb.recv('x1', 'y0')
            gvb.start('dx', 'dy')

        @at(30)
        def _():
            gva.recv('x1')
            gva.start('zx1')
            gva.recv('y0')
            gva.start('zy0')

        for e, (k, fin) in zip(G_AT, ((0, 0), (1, 0), (2, 0), (0, 1), (1, 1), (2, 1))):
            @at(e + 2)
            def _():
                g_push(k, fin)

            @at(e + 1)
            def _():
                g_add(k, fin)

            @at(e)
            def _():
                g_load(k, fin)

        q = jnp.where(j == 0, q_own, jnp.where(j == 1, q_x, jnp.where(j == 2, q_y, q_d)))
        base = pl.multiple_of(q * CH, CH)

        @pl.when(i == 0)
        def _():
            def tr(r, _):
                src = pl.ds(pl.multiple_of(base + r * 128, 128), 128)
                for a in range(2):
                    wt[:, pl.ds(pl.multiple_of(a * CH + r * 128, 128), 128)] = w_v[a, src, :].T
                return 0
            lax.fori_loop(0, CH // 128, tr, 0)

        cols = pl.ds(pl.multiple_of(i * TM, TM), TM)
        slot = n % 2

        def hcopies(slot):
            return [pltpu.make_async_copy(hbuf.at[slot, pl.ds(a * CH, CH), :],
                                          h3_hbm.at[a, pl.ds(base, CH), cols], hsem.at[slot, a]) for a in range(3)]

        @pl.when(n >= 2)
        def _():
            for cp in hcopies(slot):
                cp.wait()

        for r in range(CH // SUB):
            src = pl.ds(pl.multiple_of(base + r * SUB, 16), SUB)
            a = dotf(w_v[0, src, :], x_v[:, cols], NN)
            b = dotf(w_v[1, src, :], x_v[:, cols], NN)
            dh = dotf(w_v[2, src, :], dy_v[:, cols], NN)
            s = 1.0 / (1.0 + jnp.exp(-a))
            act = a * s
            hbuf[slot, r * SUB:(r + 1) * SUB, :] = (dh * b * s * (1.0 + a * (1.0 - s))).astype(BF16)
            hbuf[slot, CH + r * SUB:CH + (r + 1) * SUB, :] = (dh * act).astype(BF16)
            hbuf[slot, 2 * CH + r * SUB:2 * CH + (r + 1) * SUB, :] = (act * b).astype(BF16)
        for cp in hcopies(slot):
            cp.start()
        acc[:, cols] += dotf(wt[...], hbuf[slot, 0:2 * CH, :], NN)

        @pl.when(j == NC - 1)
        def _():
            x_v[:, cols] = acc[:, cols].astype(BF16)
            pltpu.make_async_copy(x_v.at[:, cols], dx_hbm.at[:, cols], xsem).start()
        return 0

    lax.fori_loop(0, NC * NI, body, 0)

    gva.recv('xf', 'yf')
    gva.start('zd0', 'zd1')
    gvb.recv('xf', 'yf')
    gvb.start('dd')
    for k in range(3):
        z_sends(k)[0].wait_recv()
        z_fwd(k).start()
    gva.recv('zx0', 'zx1', 'zy0', 'zy1')
    gva.start('dx', 'dy')
    for slot in range(2):
        for a in range(3):
            pltpu.make_async_copy(hbuf.at[slot, pl.ds(a * CH, CH), :],
                                  h3_hbm.at[a, pl.ds(0, CH), pl.ds(0, TM)], hsem.at[slot, a]).wait()
    pltpu.make_async_copy(x_v, dx_hbm, xsem).wait()
    gva.recv('zd0', 'zd1')
    gva.start('dd')
    for cp in lv:
        cp.wait()
    for cp in pv:
        cp.wait_recv()
    for k in range(3):
        z_sends(k)[1].wait_recv()
        z_fwd(k).wait_recv()
    gvb.recv('dx', 'dy', 'dd')
    gva.recv('dx', 'dy', 'dd')
    for cp in pw + pv:
        cp.wait_send()
    for g in (gw, gva, gvb):
        g.sent()
    for k in range(3):
        for m in range(2):
            px(k, m).wait_send()
            py(k, m).wait_send()
        for cp in mid_sends(k) + z_sends(k) + (z_fwd(k),):
            cp.wait_send()


def run_step(*args):
    hbm = pl.BlockSpec(memory_space=pltpu.MemorySpace.HBM)

    def out(*shape):
        return jax.ShapeDtypeStruct(shape, BF16)
    dma = pltpu.SemaphoreType.DMA
    return pl.pallas_call(
        step_kernel,
        out_shape=(out(3, F, T), out(D, T), out(3, F, D), out(2, 3, D, CH),
                   out(12, HR, CH), out(12, HR, CH), out(3, 2, QR, CH), out(3, 2, QR, CH),
                   out(3, QR, CH), out(3, QR, CH), out(3, QR, CH), out(3, QR, CH)),
        in_specs=[hbm] * 9,
        out_specs=(hbm,) * 12,
        scratch_shapes=[
            pltpu.VMEM((D, T), BF16), pltpu.VMEM((D, T), BF16), pltpu.VMEM((D, T), F32),
            pltpu.VMEM((3, F, D), BF16), pltpu.VMEM((D, 2 * CH), BF16),
            pltpu.VMEM((2, 3 * CH, TM), BF16),
            pltpu.VMEM((HR, CH), F32), pltpu.VMEM((HR, CH), BF16),
            pltpu.VMEM((HR, CH), F32), pltpu.VMEM((HR, CH), BF16), pltpu.VMEM((HR, CH), BF16),
            pltpu.VMEM((6, QR, CH), BF16), pltpu.VMEM((2, QR, CH), BF16),
            dma((8,)), dma((2, 3)), dma, dma((84,)), dma((84,)),
            dma, dma, dma((12,)), dma((3,)), dma((2, 3, 2)), dma((2, 3, 2)),
            dma((6,)), dma((2,)), dma((2, 3)), dma((2, 3)), dma((3, 3)), dma((3, 3)),
        ],
        compiler_params=pltpu.CompilerParams(collective_id=0, has_side_effects=True,
                                             vmem_limit_bytes=66_900_000),
        cost_estimate=pl.CostEstimate(flops=10 * T * D * F, bytes_accessed=200_000_000, transcendentals=T * F),
    )(*args)


def grad_kernel(x_ref, dy_ref, h3_ref, dx_ref, v_ref, sg_ref,
                dw_ref, dxo_ref, v1o_ref, v3o_ref, v2o_ref, dn_ref, gt):
    s = pl.program_id(0)
    c = lax.axis_index('fsdp') % 2
    for k, (lhs, vo) in enumerate(((x_ref, v1o_ref), (x_ref, v3o_ref), (dy_ref, v2o_ref))):
        @pl.when(s // 5 == k)
        def _():
            dxo_ref[...] = dx_ref[...]
            vo[...] = v_ref[0].T
            dw_ref[0, 0] = dotf(lhs[...], h3_ref[0], NT)

    @pl.when(s % 5 == 3)
    def _():
        for r in range(0, CH, 128):
            gt[r:r + 128, :] = (sg_ref[0, 0, :, r:r + 128].astype(F32) + sg_ref[1, 0, :, r:r + 128].astype(F32)).T
        dn_ref[0] = gt[pl.ds(pl.multiple_of(c * SH, 8), SH), :]


def run_grad(x, dy, h3, dx, v, sg):
    one = pl.Buffered(1)
    whole = pl.BlockSpec((D, T), lambda s: (0, 0), pipeline_mode=one)
    dxs = pl.BlockSpec((D // 15, T), lambda s: (s, 0))

    def vspec(k):
        return pl.BlockSpec((D, 512), lambda s: (0, jnp.clip(s - 5 * k, 0, 4)))
    return pl.pallas_call(
        grad_kernel,
        grid=(15,),
        out_shape=(jax.ShapeDtypeStruct((1, 3, D, F), F32), jax.ShapeDtypeStruct((D, T), BF16),
                   jax.ShapeDtypeStruct((D, F), BF16), jax.ShapeDtypeStruct((D, F), BF16),
                   jax.ShapeDtypeStruct((D, F), BF16), jax.ShapeDtypeStruct((3, SH, D), F32)),
        in_specs=[whole, whole, pl.BlockSpec((1, 512, T), lambda s: (s // 5, s % 5, 0)), dxs,
                  pl.BlockSpec((1, 512, D), lambda s: (s // 5, s % 5, 0)),
                  pl.BlockSpec((2, 1, D, CH), lambda s: (0, s // 5, 0, 0), pipeline_mode=one)],
        out_specs=(pl.BlockSpec((1, 1, D, 512), lambda s: (0, s // 5, 0, s % 5)), dxs, vspec(0), vspec(1), vspec(2),
                   pl.BlockSpec((1, SH, D), lambda s: (s // 5, 0, 0))),
        scratch_shapes=[pltpu.VMEM((CH, D), F32)],
        compiler_params=pltpu.CompilerParams(vmem_limit_bytes=64_000_000),
        cost_estimate=pl.CostEstimate(flops=6 * T * D * F, bytes_accessed=150_000_000, transcendentals=0),
    )(x, dy, h3, dx, v, sg)


def solution(mesh):
    def device_step(x, dy, w1, w3, w2, v1, v3, v2, g_next):
        xt, dyt = x.T, dy.T
        h3, dx, v, sg = run_step(xt, dyt, w1.T, w3.T, w2, v1.T, v3.T, v2, g_next[0])[:4]
        dw, dxo, v1o, v3o, v2o, dn = run_grad(xt, dyt, h3, dx, v, sg)
        return dxo.T, dn.transpose(0, 2, 1), dw, v1o, v3o, v2o.T

    row_spec = P(ALL_AXES, None)
    col_shard = P(None, FSDP_AXES)
    row_shard = P(FSDP_AXES, None)
    dev_spec = P(ALL_AXES, None, None, None)
    return jax.shard_map(
        device_step, mesh=mesh,
        in_specs=(row_spec, row_spec, col_shard, col_shard, row_shard, col_shard, col_shard, row_shard, dev_spec),
        out_specs=(row_spec, P(None, None, FSDP_AXES), dev_spec, P(), P(), P()),
        check_vma=False)
```

time: 291 us -> 279 us (0.959)
  Pallas kernels: 248 us -> 279 us
  local copies, waits for them, and re-layouts: 23.4 us -> 0 us
  between operations: 14.1 us -> 0.64 us
  other arithmetic: 4.3 us -> 0 us
    unnamed x3 -> x0, local copies, waits for them, and re-layouts: 23.4 us -> none
    pallas_call x1, Pallas kernels: 171 us -> 192 us  [run_step(): pl.pallas_call(step_kernel, out_shape=(out(3, F, T), out(D, T), out(3, F,...]
    pallas_call x1, Pallas kernels: 76.4 us -> 86.4 us  [run_grad(): pl.pallas_call(grad_kernel, grid=(15,), out_shape=(jax.ShapeDtypeStruct((...]
    add x1 -> x0, other arithmetic: 4.3 us -> none  [device_step(): grad_next = part.astype(F32) + other.astype(F32)]
  transfers between devices with their start and end apart: 2 -> 0, of which waited for: 0 -> 0; matrix products, arithmetic and copies ran while one was open for 0% -> 0% of each run, Pallas kernels for 85% -> 0%
where the time goes in v2:
time: 279 us
  Pallas kernels  279 us (100%)
    pallas_call x1, Pallas kernels, run_step(): pl.pallas_call(step_kernel, out_shape=(out(3, F, T), out(D, T), out(3, F,...  192 us
    pallas_call x1, Pallas kernels, run_grad(): pl.pallas_call(grad_kernel, grid=(15,), out_shape=(jax.ShapeDtypeStruct((...  86.4 us

profile of v2, /device:TPU:0, one launch (start us, length us, event | category | flops | bytes accessed | tf_op | source)
XLA Modules:
  0.0 279.3 jit_solution(13668278352850202530)
XLA Ops:
  0.6 192.2 %shard_map.136 = (bf16[3,2560,4096]{2,1,0:T(8,128)(2,1)}, bf16[960,4096]{1,0:T(8,128)(2,1)}, bf16[3,2560,960]{2,1,0:T(8,128)(2,1)}, bf16[2,3,960,640]{3,2,1,0:T(...) custom-call(bf16[960,4096]{1,0:T(8,128)(2,1)} %bitcast.11, ...), custom_call_target="tpu_custom_call" | custom-call | flops 100663296000 | bytes 200000000 | tf_op jit(solution)/shard_map/pallas_call | solution.py:489
  192.8 86.4 %shard_map.137 = (f32[1,3,960,2560]{3,2,1,0:T(8,128)}, bf16[960,4096]{1,0:T(8,128)(2,1)}, bf16[960,2560]{1,0:T(8,128)(2,1)}, bf16[960,2560]{1,0:T(8,128)(2,1)}, ...) custom-call(bf16[960,4096]{1,0:T(8,128)(2,1)} %bitcast.12, bf16[960,4096]{1,0:T(8,128)(2,1)} %bitcast.14, ...), custom_call_target="tpu_custom_call" | custom-call | flops 60397977600 | bytes 150000000 | tf_op jit(solution)/shard_map/pallas_call | solution.py:538

commit v3 on v2

--- a/solution.py
+++ b/solution.py
@@ -22,8 +22,8 @@
 SUB = 320
 HR = D // 2
 QR = HR // 2
-S2 = 3
-G_AT = (13, 16, 18, 20, 23, 25)
+S2 = 2
+G_AT = (9, 12, 15, 17, 19, 22)
 
 NN = (((1,), (0,)), ((), ()))
 NT = (((1,), (1,)), ((), ()))
@@ -34,9 +34,9 @@
 
 
 def step_kernel(x_hbm, dy_hbm, w1_hbm, w3_hbm, w2_hbm, v1_hbm, v3_hbm, v2_hbm, g_hbm,
-                h3_hbm, dx_hbm, v_out, sg, r1, pp, rx, ry, rx2, ry2, sx, sy,
-                x_v, dy_v, acc, w_v, wt, hbuf, gin1, gout1, gin2, rin, gout2, ab, ob,
-                lsem, hsem, xsem, send, recv, g1l, g1s, g1r, g2l, gps, gpr, abl, obs, gms, gmr, zs, zr):
+                h3_hbm, dw_hbm, dx_hbm, v_out, sg, r1, pp, rx, ry, rx2, ry2, sx, sy,
+                x_v, dy_v, acc, w_v, wt, hbuf, h_v, dacc, gin1, gout1, gin2, rin, gout2, ab, ob,
+                lsem, hsem, xsem, wsem, send, recv, g1l, g1s, g1r, g2l, gps, gpr, abl, obs, gms, gmr, zs, zr):
     z = lax.axis_index('dp')
     y = lax.axis_index('col')
     fs = lax.axis_index('fsdp')
@@ -119,28 +119,29 @@
         return pl.ds(pl.multiple_of(q * CH, 128), CH)
 
     def unit(u):
-        m = u % 4
+        k = jnp.where(u < 9, u // 3, u - 9)
+        m = jnp.where(u < 9, u % 3, 3)
         q = jnp.where(m == 0, q_d, jnp.where(m == 1, q_x, jnp.where(m == 2, q_y, q_own)))
-        return u // 4, cols_of(q)
+        return k, 4 * k + m, cols_of(q)
 
     def half(h):
         return pl.ds(pl.multiple_of(h * HR, 16), HR)
 
     def g1_load(u):
-        k, cq = unit(u)
+        k, _, cq = unit(u)
         return pltpu.make_async_copy(g_hbm.at[k, half(1 - c), cq], gin1, g1l)
 
     def g1_send(u):
-        k, _ = unit(u)
         return rdma(gout1, r1.at[u], g1s, g1r.at[u], partner)
 
     def g2_loads(u):
-        k, cq = unit(u)
+        k, _, cq = unit(u)
         return (pltpu.make_async_copy(g_hbm.at[k, half(c), cq], gin2, g2l.at[0]),
                 pltpu.make_async_copy(r1.at[u], rin, g2l.at[1]))
 
     def g2_out(u):
-        return pltpu.make_async_copy(gout2, pp.at[u], g2l.at[2])
+        _, km, _ = unit(u)
+        return pltpu.make_async_copy(gout2, pp.at[km], g2l.at[2])
 
     def px(k, m):
         return rdma(pp.at[4 * k + m, pl.ds(0, QR), :], rx.at[k, m], gps.at[0, k, m], gpr.at[0, k, m], xnbr)
@@ -154,11 +155,8 @@
             g1_send(u - 1).wait_send()
         g1_load(u).wait()
 
-        def cast(r, _):
-            rows = pl.ds(pl.multiple_of(r * 48, 16), 48)
-            gout1[rows, :] = gin1[rows, :].astype(BF16)
-            return 0
-        lax.fori_loop(0, HR // 48, cast, 0)
+        for r in range(0, HR, 48):
+            gout1[r:r + 48, :] = gin1[r:r + 48, :].astype(BF16)
         g1_send(u).start()
 
         @pl.when(u < 11)
@@ -167,18 +165,18 @@
 
     def g_sends(u):
         g2_out(u).wait()
-        k = u // 4
-
-        @pl.when(u % 4 == 0)
+        k = u // 3
+
+        @pl.when((u < 9) & (u % 3 == 0))
         def _():
             px(k, 0).start()
             py(k, 0).start()
 
-        @pl.when(u % 4 == 1)
+        @pl.when((u < 9) & (u % 3 == 1))
         def _():
             px(k, 1).start()
 
-        @pl.when(u % 4 == 2)
+        @pl.when((u < 9) & (u % 3 == 2))
         def _():
             py(k, 1).start()
 
@@ -186,11 +184,8 @@
         for cp in g2_loads(u):
             cp.wait()
 
-        def add(r, _):
-            rows = pl.ds(pl.multiple_of(r * 48, 16), 48)
-            gout2[rows, :] = (gin2[rows, :].astype(BF16).astype(F32) + rin[rows, :].astype(F32)).astype(BF16)
-            return 0
-        lax.fori_loop(0, HR // 48, add, 0)
+        for r in range(0, HR, 48):
+            gout2[r:r + 48, :] = (gin2[r:r + 48, :].astype(BF16).astype(F32) + rin[r:r + 48, :].astype(F32)).astype(BF16)
         g2_out(u).start()
 
         @pl.when(u < 11)
@@ -309,80 +304,137 @@
         def _():
             g_stage2(n - S2)
 
-        @at(3)
+        @at(2)
         def _():
             gw.recv('x0')
-            gw.start('zx0', 'yf')
+            gw.start('zx0')
+            gw.start('yf')
             gw.recv('y1')
             gw.start('xf')
 
+        @at(4)
+        def _():
+            gw.recv('x1')
+            gw.start('zx1')
+            gw.recv('y0')
+
         @at(5)
         def _():
-            gw.recv('x1')
-            gw.start('zx1', 'zy1')
-            gw.recv('y0')
+            gw.start('zy1')
             gw.start('zy0')
             for cp in lv + pv:
                 cp.start()
 
+        @at(7)
+        def _():
+            gw.recv('zx0')
+            gw.recv('zx1')
+            gw.start('dx')
+
         @at(8)
         def _():
-            gw.recv('zx0', 'zx1')
-            gw.start('dx')
             gw.recv('dx')
 
+        @at(10)
+        def _():
+            gw.recv('xf')
+            gw.recv('yf')
+            gw.start('zd0')
+            gw.start('zd1')
+
         @at(12)
         def _():
             g1_send(11).wait_send()
-            gw.recv('xf', 'yf')
-            gw.start('zd0', 'zd1')
-
-        @at(15)
-        def _():
-            gw.recv('zy0', 'zy1')
+
+        @at(13)
+        def _():
+            gvb.start('x0')
+            gvb.start('y1')
+
+        @at(14)
+        def _():
+            gw.recv('zy0')
+            gw.recv('zy1')
             gw.start('dy')
-            gvb.start('x0', 'y1')
 
         @at(16)
         def _():
             gw.recv('dy')
+            gvb.start('x1')
+            gvb.start('y0')
 
         @at(18)
         def _():
-            gvb.start('x1', 'y0')
+            gva.start('x0')
+            gva.start('y1')
+            gva.start('x1')
+            gva.start('y0')
+
+        @at(19)
+        def _():
+            gw.recv('zd0')
+            gw.recv('zd1')
+            gw.start('dd')
 
         @at(20)
         def _():
-            gva.start('x0', 'y1', 'x1', 'y0')
-
-        @at(22)
-        def _():
-            gw.recv('zd0', 'zd1')
-            gw.start('dd')
-
-        @at(24)
-        def _():
-            gw.recv('dd')
             gvb.recv('x0')
             gvb.start('yf')
             gvb.recv('y1')
             gvb.start('xf')
 
-        @at(28)
-        def _():
+        @at(23)
+        def _():
+            gvb.recv('x1')
+            gvb.recv('y0')
+            gvb.start('dx')
+            gvb.start('dy')
+
+        @at(24)
+        def _():
+            gw.recv('dd')
             gva.recv('x0')
-            gva.start('yf', 'zx0')
+            gva.start('yf')
+            gva.start('zx0')
             gva.recv('y1')
-            gva.start('xf', 'zy1')
-            gvb.recv('x1', 'y0')
-            gvb.start('dx', 'dy')
-
-        @at(30)
-        def _():
+            gva.start('xf')
+            gva.start('zy1')
             gva.recv('x1')
             gva.start('zx1')
             gva.recv('y0')
             gva.start('zy0')
+
+        @at(26)
+        def _():
+            gvb.recv('xf')
+            gvb.recv('yf')
+            gvb.start('dd')
+
+        @at(27)
+        def _():
+            gva.recv('xf')
+            gva.recv('yf')
+            gva.start('zd0')
+            gva.start('zd1')
+            z_sends(0)[0].wait_recv()
+            z_fwd(0).start()
+
+        @at(29)
+        def _():
+            gva.recv('zx0')
+            gva.recv('zx1')
+            gva.recv('zy0')
+            gva.recv('zy1')
+            gva.start('dx')
+            gva.start('dy')
+            z_sends(1)[0].wait_recv()
+            z_fwd(1).start()
+
+        @at(31)
+        def _():
+            gva.recv('zd0')
+            gva.recv('zd1')
+            gva.start('dd')
 
         for e, (k, fin) in zip(G_AT, ((0, 0), (1, 0), (2, 0), (0, 1), (1, 1), (2, 1))):
             @at(e + 2)
@@ -414,7 +466,13 @@
 
         def hcopies(slot):
             return [pltpu.make_async_copy(hbuf.at[slot, pl.ds(a * CH, CH), :],
-                                          h3_hbm.at[a, pl.ds(base, CH), cols], hsem.at[slot, a]) for a in range(3)]
+                                          h3_hbm.at[a, pl.ds(base, CH), cols], hsem.at[slot, a]) for a in range(2)]
+
+        dw_copy = pltpu.make_async_copy(dacc, dw_hbm.at[:, pl.ds(base, CH)], wsem)
+
+        @pl.when((i == 0) & (j > 0))
+        def _():
+            dw_copy.wait()
 
         @pl.when(n >= 2)
         def _():
@@ -430,10 +488,15 @@
             act = a * s
             hbuf[slot, r * SUB:(r + 1) * SUB, :] = (dh * b * s * (1.0 + a * (1.0 - s))).astype(BF16)
             hbuf[slot, CH + r * SUB:CH + (r + 1) * SUB, :] = (dh * act).astype(BF16)
-            hbuf[slot, 2 * CH + r * SUB:2 * CH + (r + 1) * SUB, :] = (act * b).astype(BF16)
+            h_v[r * SUB:(r + 1) * SUB, :] = (act * b).astype(BF16)
         for cp in hcopies(slot):
             cp.start()
-        acc[:, cols] += dotf(wt[...], hbuf[slot, 0:2 * CH, :], NN)
+        acc[:, cols] += dotf(wt[...], hbuf[slot], NN)
+        dacc[...] = jnp.where(i == 0, 0.0, dacc[...]) + dotf(dy_v[:, cols], h_v[...], NT)
+
+        @pl.when(i == NI - 1)
+        def _():
+            dw_copy.start()
 
         @pl.when(j == NC - 1)
         def _():
@@ -443,22 +506,14 @@
 
     lax.fori_loop(0, NC * NI, body, 0)
 
-    gva.recv('xf', 'yf')
-    gva.start('zd0', 'zd1')
-    gvb.recv('xf', 'yf')
-    gvb.start('dd')
-    for k in range(3):
-        z_sends(k)[0].wait_recv()
-        z_fwd(k).start()
-    gva.recv('zx0', 'zx1', 'zy0', 'zy1')
-    gva.start('dx', 'dy')
+    z_sends(2)[0].wait_recv()
+    z_fwd(2).start()
+    pltpu.make_async_copy(dacc, dw_hbm.at[:, pl.ds(0, CH)], wsem).wait()
     for slot in range(2):
-        for a in range(3):
+        for a in range(2):
             pltpu.make_async_copy(hbuf.at[slot, pl.ds(a * CH, CH), :],
                                   h3_hbm.at[a, pl.ds(0, CH), pl.ds(0, TM)], hsem.at[slot, a]).wait()
     pltpu.make_async_copy(x_v, dx_hbm, xsem).wait()
-    gva.recv('zd0', 'zd1')
-    gva.start('dd')
     for cp in lv:
         cp.wait()
     for cp in pv:
@@ -483,80 +538,107 @@
 def run_step(*args):
     hbm = pl.BlockSpec(memory_space=pltpu.MemorySpace.HBM)
 
-    def out(*shape):
-        return jax.ShapeDtypeStruct(shape, BF16)
+    def out(*shape, dtype=BF16):
+        return jax.ShapeDtypeStruct(shape, dtype)
     dma = pltpu.SemaphoreType.DMA
     return pl.pallas_call(
         step_kernel,
-        out_shape=(out(3, F, T), out(D, T), out(3, F, D), out(2, 3, D, CH),
+        out_shape=(out(2, F, T), out(D, F, dtype=F32), out(D, T), out(3, F, D), out(2, 3, D, CH),
                    out(12, HR, CH), out(12, HR, CH), out(3, 2, QR, CH), out(3, 2, QR, CH),
                    out(3, QR, CH), out(3, QR, CH), out(3, QR, CH), out(3, QR, CH)),
         in_specs=[hbm] * 9,
-        out_specs=(hbm,) * 12,
+        out_specs=(hbm,) * 13,
         scratch_shapes=[
             pltpu.VMEM((D, T), BF16), pltpu.VMEM((D, T), BF16), pltpu.VMEM((D, T), F32),
             pltpu.VMEM((3, F, D), BF16), pltpu.VMEM((D, 2 * CH), BF16),
-            pltpu.VMEM((2, 3 * CH, TM), BF16),
+            pltpu.VMEM((2, 2 * CH, TM), BF16), pltpu.VMEM((CH, TM), BF16), pltpu.VMEM((D, CH), F32),
             pltpu.VMEM((HR, CH), F32), pltpu.VMEM((HR, CH), BF16),
             pltpu.VMEM((HR, CH), F32), pltpu.VMEM((HR, CH), BF16), pltpu.VMEM((HR, CH), BF16),
             pltpu.VMEM((6, QR, CH), BF16), pltpu.VMEM((2, QR, CH), BF16),
-            dma((8,)), dma((2, 3)), dma, dma((84,)), dma((84,)),
+            dma((8,)), dma((2, 2)), dma, dma, dma((84,)), dma((84,)),
             dma, dma, dma((12,)), dma((3,)), dma((2, 3, 2)), dma((2, 3, 2)),
             dma((6,)), dma((2,)), dma((2, 3)), dma((2, 3)), dma((3, 3)), dma((3, 3)),
         ],
         compiler_params=pltpu.CompilerParams(collective_id=0, has_side_effects=True,
                                              vmem_limit_bytes=66_900_000),
-        cost_estimate=pl.CostEstimate(flops=10 * T * D * F, bytes_accessed=200_000_000, transcendentals=T * F),
+        cost_estimate=pl.CostEstimate(flops=12 * T * D * F, bytes_accessed=200_000_000, transcendentals=T * F),
     )(*args)
 
 
-def grad_kernel(x_ref, dy_ref, h3_ref, dx_ref, v_ref, sg_ref,
-                dw_ref, dxo_ref, v1o_ref, v3o_ref, v2o_ref, dn_ref, gt):
+def grad_kernel(x_ref, h3_ref, dwt_ref, dx_ref, v_ref, sg_ref,
+                dw_hbm, dxo_ref, v1o_ref, v3o_ref, v2o_ref, dn_ref, ob, gt, osem, csem):
     s = pl.program_id(0)
     c = lax.axis_index('fsdp') % 2
-    for k, (lhs, vo) in enumerate(((x_ref, v1o_ref), (x_ref, v3o_ref), (dy_ref, v2o_ref))):
-        @pl.when(s // 5 == k)
-        def _():
-            dxo_ref[...] = dx_ref[...]
-            vo[...] = v_ref[0].T
-            dw_ref[0, 0] = dotf(lhs[...], h3_ref[0], NT)
-
-    @pl.when(s % 5 == 3)
+
+    def out(s):
+        return pltpu.make_async_copy(
+            ob.at[s % 2], dw_hbm.at[0, s // 5, :, pl.ds(pl.multiple_of(s % 5 * 512, 512), 512)], osem.at[s % 2])
+
+    def third(s):
+        return pltpu.make_async_copy(dwt_ref, dw_hbm.at[0, 2, pl.ds(pl.multiple_of(s * 96, 8), 96), :], csem)
+
+    third(s).start()
+
+    @pl.when(s >= 2)
     def _():
-        for r in range(0, CH, 128):
-            gt[r:r + 128, :] = (sg_ref[0, 0, :, r:r + 128].astype(F32) + sg_ref[1, 0, :, r:r + 128].astype(F32)).T
-        dn_ref[0] = gt[pl.ds(pl.multiple_of(c * SH, 8), SH), :]
-
-
-def run_grad(x, dy, h3, dx, v, sg):
+        out(s - 2).wait()
+
+    def main():
+        dxo_ref[...] = dx_ref[...]
+        for a, vo in enumerate((v1o_ref, v3o_ref, v2o_ref)):
+            vo[...] = v_ref[a].T
+        ob[s % 2] = dotf(x_ref[...], h3_ref[0], NT)
+
+    @pl.when(s % 2 == 0)
+    def _():
+        rows = pl.ds(pl.multiple_of(s // 2 * 128, 128), 128)
+        for k in range(3):
+            gt[k, rows, :] = (sg_ref[0, k].astype(F32) + sg_ref[1, k].astype(F32)).T
+        main()
+
+    @pl.when(s % 2 == 1)
+    def _():
+        main()
+
+    out(s).start()
+    third(s).wait()
+
+    @pl.when(s == 9)
+    def _():
+        dn_ref[...] = gt[:, pl.ds(pl.multiple_of(c * SH, 8), SH), :]
+        out(8).wait()
+        out(9).wait()
+
+
+def run_grad(x, h3, dwt, dx, v, sg):
     one = pl.Buffered(1)
-    whole = pl.BlockSpec((D, T), lambda s: (0, 0), pipeline_mode=one)
-    dxs = pl.BlockSpec((D // 15, T), lambda s: (s, 0))
-
-    def vspec(k):
-        return pl.BlockSpec((D, 512), lambda s: (0, jnp.clip(s - 5 * k, 0, 4)))
+    dxs = pl.BlockSpec((D // 10, T), lambda s: (s, 0))
+    vs = pl.BlockSpec((D, 256), lambda s: (0, s))
     return pl.pallas_call(
         grad_kernel,
-        grid=(15,),
+        grid=(10,),
         out_shape=(jax.ShapeDtypeStruct((1, 3, D, F), F32), jax.ShapeDtypeStruct((D, T), BF16),
                    jax.ShapeDtypeStruct((D, F), BF16), jax.ShapeDtypeStruct((D, F), BF16),
                    jax.ShapeDtypeStruct((D, F), BF16), jax.ShapeDtypeStruct((3, SH, D), F32)),
-        in_specs=[whole, whole, pl.BlockSpec((1, 512, T), lambda s: (s // 5, s % 5, 0)), dxs,
-                  pl.BlockSpec((1, 512, D), lambda s: (s // 5, s % 5, 0)),
-                  pl.BlockSpec((2, 1, D, CH), lambda s: (0, s // 5, 0, 0), pipeline_mode=one)],
-        out_specs=(pl.BlockSpec((1, 1, D, 512), lambda s: (0, s // 5, 0, s % 5)), dxs, vspec(0), vspec(1), vspec(2),
-                   pl.BlockSpec((1, SH, D), lambda s: (s // 5, 0, 0))),
-        scratch_shapes=[pltpu.VMEM((CH, D), F32)],
+        in_specs=[pl.BlockSpec((D, T), lambda s: (0, 0), pipeline_mode=one),
+                  pl.BlockSpec((1, 512, T), lambda s: (s // 5, s % 5, 0)),
+                  pl.BlockSpec((D // 10, F), lambda s: (s, 0)), dxs,
+                  pl.BlockSpec((3, 256, D), lambda s: (0, s, 0)),
+                  pl.BlockSpec((2, 3, D, 128), lambda s: (0, 0, 0, s // 2))],
+        out_specs=(pl.BlockSpec(memory_space=pltpu.MemorySpace.HBM), dxs, vs, vs, vs,
+                   pl.BlockSpec((3, SH, D), lambda s: (0, 0, 0), pipeline_mode=one)),
+        scratch_shapes=[pltpu.VMEM((2, D, 512), F32), pltpu.VMEM((3, CH, D), F32),
+                        pltpu.SemaphoreType.DMA((2,)), pltpu.SemaphoreType.DMA],
         compiler_params=pltpu.CompilerParams(vmem_limit_bytes=64_000_000),
-        cost_estimate=pl.CostEstimate(flops=6 * T * D * F, bytes_accessed=150_000_000, transcendentals=0),
-    )(x, dy, h3, dx, v, sg)
+        cost_estimate=pl.CostEstimate(flops=4 * T * D * F, bytes_accessed=150_000_000, transcendentals=0),
+    )(x, h3, dwt, dx, v, sg)
 
 
 def solution(mesh):
     def device_step(x, dy, w1, w3, w2, v1, v3, v2, g_next):
         xt, dyt = x.T, dy.T
-        h3, dx, v, sg = run_step(xt, dyt, w1.T, w3.T, w2, v1.T, v3.T, v2, g_next[0])[:4]
-        dw, dxo, v1o, v3o, v2o, dn = run_grad(xt, dyt, h3, dx, v, sg)
+        h3, dwt, dx, v, sg = run_step(xt, dyt, w1.T, w3.T, w2, v1.T, v3.T, v2, g_next[0])[:5]
+        dw, dxo, v1o, v3o, v2o, dn = run_grad(xt, h3, dwt, dx, v, sg)
         return dxo.T, dn.transpose(0, 2, 1), dw, v1o, v3o, v2o.T
 
     row_spec = P(ALL_AXES, None)

time: 279 us -> 243 us (0.87)
  Pallas kernels: 279 us -> 242 us
    pallas_call x2, Pallas kernels: 279 us -> 242 us  [the longest x1 183 us: run_step(): pl.pallas_call(step_kernel, out_shape=(out(2, F, T), out(D, F, dtype=F32)...]
where the time goes in v3:
time: 243 us
  Pallas kernels  242 us (100%)
    pallas_call x1, Pallas kernels, run_step(): pl.pallas_call(step_kernel, out_shape=(out(2, F, T), out(D, F, dtype=F32)...  183 us
    pallas_call x1, Pallas kernels, run_grad(): pl.pallas_call(grad_kernel, grid=(10,), out_shape=(jax.ShapeDtypeStruct((...  58.5 us

profile of v3, /device:TPU:0, one launch (start us, length us, event | category | flops | bytes accessed | tf_op | source)
XLA Modules:
  0.0 242.7 jit_solution(15666297691255188648)
XLA Ops:
  0.6 183.4 %shard_map.136 = (bf16[2,2560,4096]{2,1,0:T(8,128)(2,1)}, f32[960,2560]{1,0:T(8,128)}, bf16[960,4096]{1,0:T(8,128)(2,1)}, bf16[3,2560,960]{2,1,0:T(8,128)(2,1)},...) custom-call(bf16[960,4096]{1,0:T(8,128)(2,1)} %bitcast.12, ...), custom_call_target="tpu_custom_call" | custom-call | flops 120795955200 | bytes 200000000 | tf_op jit(solution)/shard_map/pallas_call | solution.py:544
  184.0 58.5 %shard_map.137 = (f32[1,3,960,2560]{3,2,1,0:T(8,128)}, bf16[960,4096]{1,0:T(8,128)(2,1)}, bf16[960,2560]{1,0:T(8,128)(2,1)}, bf16[960,2560]{1,0:T(8,128)(2,1)}, ...) custom-call(bf16[960,4096]{1,0:T(8,128)(2,1)} %bitcast.13, bf16[2,2560,4096]{2,1,0:T(8,128)(2,1)} %get-tuple-element.17.h3_ref, ...), custom_call_target="tpu_custom_call" | custom-call | flops 40265318400 | bytes 150000000 | tf_op jit(solution)/shard_map/pallas_call | solution.py:617

commit v4 on v3

--- a/solution.py
+++ b/solution.py
@@ -1,3 +1,5 @@
+import functools
+
 import jax
 import jax.numpy as jnp
 from jax import lax
@@ -22,8 +24,9 @@
 SUB = 320
 HR = D // 2
 QR = HR // 2
+RB = D // 10
 S2 = 2
-G_AT = (9, 12, 15, 17, 19, 22)
+G_AT = (9, 12, 15, 18, 21, 24)
 
 NN = (((1,), (0,)), ((), ()))
 NT = (((1,), (1,)), ((), ()))
@@ -36,7 +39,7 @@
 def step_kernel(x_hbm, dy_hbm, w1_hbm, w3_hbm, w2_hbm, v1_hbm, v3_hbm, v2_hbm, g_hbm,
                 h3_hbm, dw_hbm, dx_hbm, v_out, sg, r1, pp, rx, ry, rx2, ry2, sx, sy,
                 x_v, dy_v, acc, w_v, wt, hbuf, h_v, dacc, gin1, gout1, gin2, rin, gout2, ab, ob,
-                lsem, hsem, xsem, wsem, send, recv, g1l, g1s, g1r, g2l, gps, gpr, abl, obs, gms, gmr, zs, zr):
+                lsem, xl, hsem, xsem, wsem, send, recv, g1l, g1s, g1r, g2l, gps, gpr, abl, obs, gms, gmr, zs, zr):
     z = lax.axis_index('dp')
     y = lax.axis_index('col')
     fs = lax.axis_index('fsdp')
@@ -113,7 +116,11 @@
     pv = [remote(v_hbm[a], gva.blk(a, q_own, 0, SH), partner, 81 + a) for a in range(3)]
     lw = [local(w_hbm[a], gw.blk(a, q_own, 0, SH), a) for a in range(3)]
     lv = [local(v_hbm[a], gva.blk(a, q_own, 0, SH), 3 + a) for a in range(3)]
-    lx = [local(x_hbm, x_v, 6), local(dy_hbm, dy_v, 7)]
+
+    def lx(i):
+        cols = pl.ds(pl.multiple_of(i * TM, TM), TM)
+        return [pltpu.make_async_copy(src.at[:, cols], dst.at[:, cols], xl.at[k, i])
+                for k, (src, dst) in enumerate(((x_hbm, x_v), (dy_hbm, dy_v)))]
 
     def cols_of(q):
         return pl.ds(pl.multiple_of(q * CH, 128), CH)
@@ -150,9 +157,6 @@
         return rdma(pp.at[4 * k + 2 * m, pl.ds(QR, QR), :], ry.at[k, m], gps.at[1, k, m], gpr.at[1, k, m], ynbr)
 
     def g_stage1(u):
-        @pl.when(u > 0)
-        def _():
-            g1_send(u - 1).wait_send()
         g1_load(u).wait()
 
         for r in range(0, HR, 48):
@@ -258,7 +262,7 @@
         for cp in (z_sends(k) if fin else mid_sends(k)):
             cp.start()
 
-    for cp in lw + lx:
+    for cp in lw + lx(0):
         cp.start()
     g1_load(0).start()
     bar = pltpu.get_barrier_semaphore()
@@ -268,13 +272,10 @@
     for cp in pw:
         cp.start()
     gw.start('x0', 'y1', 'x1', 'y0')
-
-    def zero(r, _):
-        acc[pl.ds(pl.multiple_of(r * 16, 16), 16), :] = jnp.zeros((16, T), F32)
-        return 0
-    lax.fori_loop(0, D // 16, zero, 0)
-
-    for cp in lw + lx:
+    for i in range(1, NI):
+        for cp in lx(i):
+            cp.start()
+    for cp in lw:
         cp.wait()
     for cp in pw:
         cp.wait_recv()
@@ -283,32 +284,41 @@
         j = n // NI
         i = n % NI
 
+        @pl.when((n > 0) & (n <= 12))
+        def _():
+            g1_send(n - 1).wait_send()
+
+        @pl.when(n <= S2 + 12)
+        def _():
+            @pl.when(n < 12)
+            def _():
+                g_stage1(n)
+
+            @pl.when(n == S2 - 1)
+            def _():
+                g1_send(0).wait_recv()
+                for cp in g2_loads(0):
+                    cp.start()
+
+            @pl.when(n > S2)
+            def _():
+                g_sends(n - S2 - 1)
+
+            @pl.when((n >= S2) & (n < S2 + 12))
+            def _():
+                g_stage2(n - S2)
+
+        steps = {}
+
         def at(k):
-            return pl.when(n == k)
-
-        @pl.when(n < 12)
-        def _():
-            g_stage1(n)
-
-        @at(S2 - 1)
-        def _():
-            g1_send(0).wait_recv()
-            for cp in g2_loads(0):
-                cp.start()
-
-        @pl.when((n > S2) & (n <= S2 + 12))
-        def _():
-            g_sends(n - S2 - 1)
-
-        @pl.when((n >= S2) & (n < S2 + 12))
-        def _():
-            g_stage2(n - S2)
+            def put(f):
+                steps.setdefault(k, []).append(f)
+            return put
 
         @at(2)
         def _():
             gw.recv('x0')
-            gw.start('zx0')
-            gw.start('yf')
+            gw.start('zx0', 'yf')
             gw.recv('y1')
             gw.start('xf')
 
@@ -320,15 +330,17 @@
 
         @at(5)
         def _():
-            gw.start('zy1')
-            gw.start('zy0')
+            gw.start('zy1', 'zy0')
             for cp in lv + pv:
                 cp.start()
 
+        @at(6)
+        def _():
+            gva.start('x0', 'y1', 'x1', 'y0')
+
         @at(7)
         def _():
-            gw.recv('zx0')
-            gw.recv('zx1')
+            gw.recv('zx0', 'zx1')
             gw.start('dx')
 
         @at(8)
@@ -337,117 +349,95 @@
 
         @at(10)
         def _():
-            gw.recv('xf')
-            gw.recv('yf')
-            gw.start('zd0')
-            gw.start('zd1')
-
-        @at(12)
-        def _():
-            g1_send(11).wait_send()
-
-        @at(13)
-        def _():
-            gvb.start('x0')
-            gvb.start('y1')
+            gw.recv('xf', 'yf')
+            gw.start('zd0', 'zd1')
+
+        @at(11)
+        def _():
+            gva.recv('x0')
+            gva.start('yf', 'zx0')
+            gva.recv('y1')
+            gva.start('xf', 'zy1')
+            gva.recv('x1')
+            gva.start('zx1')
+            gva.recv('y0')
+            gva.start('zy0')
 
         @at(14)
         def _():
-            gw.recv('zy0')
-            gw.recv('zy1')
+            gw.recv('zy0', 'zy1')
             gw.start('dy')
 
         @at(16)
         def _():
             gw.recv('dy')
-            gvb.start('x1')
-            gvb.start('y0')
-
-        @at(18)
-        def _():
-            gva.start('x0')
-            gva.start('y1')
-            gva.start('x1')
-            gva.start('y0')
+            gva.recv('xf', 'yf')
+            gva.start('zd0', 'zd1')
+            gvb.start('x0', 'y1')
 
         @at(19)
         def _():
-            gw.recv('zd0')
-            gw.recv('zd1')
+            gw.recv('zd0', 'zd1')
             gw.start('dd')
+            gvb.start('x1', 'y0')
 
         @at(20)
+        def _():
+            gva.recv('zx0', 'zx1', 'zy0', 'zy1')
+            gva.start('dx', 'dy')
+            gva.recv('zd0', 'zd1')
+            gva.start('dd')
+
+        @at(23)
         def _():
             gvb.recv('x0')
             gvb.start('yf')
             gvb.recv('y1')
             gvb.start('xf')
 
-        @at(23)
-        def _():
-            gvb.recv('x1')
-            gvb.recv('y0')
-            gvb.start('dx')
-            gvb.start('dy')
-
         @at(24)
         def _():
             gw.recv('dd')
-            gva.recv('x0')
-            gva.start('yf')
-            gva.start('zx0')
-            gva.recv('y1')
-            gva.start('xf')
-            gva.start('zy1')
-            gva.recv('x1')
-            gva.start('zx1')
-            gva.recv('y0')
-            gva.start('zy0')
-
-        @at(26)
-        def _():
-            gvb.recv('xf')
-            gvb.recv('yf')
-            gvb.start('dd')
-
-        @at(27)
-        def _():
-            gva.recv('xf')
-            gva.recv('yf')
-            gva.start('zd0')
-            gva.start('zd1')
+
+        @at(25)
+        def _():
             z_sends(0)[0].wait_recv()
             z_fwd(0).start()
 
-        @at(29)
-        def _():
-            gva.recv('zx0')
-            gva.recv('zx1')
-            gva.recv('zy0')
-            gva.recv('zy1')
-            gva.start('dx')
-            gva.start('dy')
+        @at(27)
+        def _():
+            gvb.recv('x1', 'y0')
+            gvb.start('dx', 'dy')
+
+        @at(28)
+        def _():
             z_sends(1)[0].wait_recv()
             z_fwd(1).start()
 
+        @at(30)
+        def _():
+            gvb.recv('xf', 'yf')
+            gvb.start('dd')
+
         @at(31)
         def _():
-            gva.recv('zd0')
-            gva.recv('zd1')
-            gva.start('dd')
+            z_sends(2)[0].wait_recv()
+            z_fwd(2).start()
 
         for e, (k, fin) in zip(G_AT, ((0, 0), (1, 0), (2, 0), (0, 1), (1, 1), (2, 1))):
-            @at(e + 2)
+            at(e + 2)(functools.partial(g_push, k, fin))
+            at(e + 1)(functools.partial(g_add, k, fin))
+            at(e)(functools.partial(g_load, k, fin))
+
+        for jj in range(NC):
+            @pl.when(j == jj)
             def _():
-                g_push(k, fin)
-
-            @at(e + 1)
-            def _():
-                g_add(k, fin)
-
-            @at(e)
-            def _():
-                g_load(k, fin)
+                for ii in range(NI):
+                    if jj * NI + ii in steps:
+                        @pl.when(i == ii)
+                        def _():
+                            for f in steps[jj * NI + ii]:
+                                f()
 
         q = jnp.where(j == 0, q_own, jnp.where(j == 1, q_x, jnp.where(j == 2, q_y, q_d)))
         base = pl.multiple_of(q * CH, CH)
@@ -467,6 +457,11 @@
         def hcopies(slot):
             return [pltpu.make_async_copy(hbuf.at[slot, pl.ds(a * CH, CH), :],
                                           h3_hbm.at[a, pl.ds(base, CH), cols], hsem.at[slot, a]) for a in range(2)]
+
+        @pl.when(j == 0)
+        def _():
+            for cp in lx(i):
+                cp.wait()
 
         dw_copy = pltpu.make_async_copy(dacc, dw_hbm.at[:, pl.ds(base, CH)], wsem)
 
@@ -491,7 +486,7 @@
             h_v[r * SUB:(r + 1) * SUB, :] = (act * b).astype(BF16)
         for cp in hcopies(slot):
             cp.start()
-        acc[:, cols] += dotf(wt[...], hbuf[slot], NN)
+        acc[:, cols] = jnp.where(j == 0, 0.0, acc[:, cols]) + dotf(wt[...], hbuf[slot], NN)
         dacc[...] = jnp.where(i == 0, 0.0, dacc[...]) + dotf(dy_v[:, cols], h_v[...], NT)
 
         @pl.when(i == NI - 1)
@@ -506,8 +501,6 @@
 
     lax.fori_loop(0, NC * NI, body, 0)
 
-    z_sends(2)[0].wait_recv()
-    z_fwd(2).start()
     pltpu.make_async_copy(dacc, dw_hbm.at[:, pl.ds(0, CH)], wsem).wait()
     for slot in range(2):
         for a in range(2):
@@ -555,7 +548,7 @@
             pltpu.VMEM((HR, CH), F32), pltpu.VMEM((HR, CH), BF16),
             pltpu.VMEM((HR, CH), F32), pltpu.VMEM((HR, CH), BF16), pltpu.VMEM((HR, CH), BF16),
             pltpu.VMEM((6, QR, CH), BF16), pltpu.VMEM((2, QR, CH), BF16),
-            dma((8,)), dma((2, 2)), dma, dma, dma((84,)), dma((84,)),
+            dma((6,)), dma((2, NI)), dma((2, 2)), dma, dma, dma((84,)), dma((84,)),
             dma, dma, dma((12,)), dma((3,)), dma((2, 3, 2)), dma((2, 3, 2)),
             dma((6,)), dma((2,)), dma((2, 3)), dma((2, 3)), dma((3, 3)), dma((3, 3)),
         ],
@@ -565,8 +558,9 @@
     )(*args)
 
 
-def grad_kernel(x_ref, h3_ref, dwt_ref, dx_ref, v_ref, sg_ref,
-                dw_hbm, dxo_ref, v1o_ref, v3o_ref, v2o_ref, dn_ref, ob, gt, osem, csem):
+def grad_kernel(x_hbm, h3_ref, dwt_hbm, dx_hbm, v_ref, sg_ref,
+                dw_hbm, dxo_hbm, v1o_ref, v3o_ref, v2o_ref, dn_ref,
+                xs, ob, gt, tb, db, xsem, osem, isem, esem):
     s = pl.program_id(0)
     c = lax.axis_index('fsdp') % 2
 
@@ -574,61 +568,101 @@
         return pltpu.make_async_copy(
             ob.at[s % 2], dw_hbm.at[0, s // 5, :, pl.ds(pl.multiple_of(s % 5 * 512, 512), 512)], osem.at[s % 2])
 
-    def third(s):
-        return pltpu.make_async_copy(dwt_ref, dw_hbm.at[0, 2, pl.ds(pl.multiple_of(s * 96, 8), 96), :], csem)
-
-    third(s).start()
+    def rows(s):
+        return pl.ds(pl.multiple_of(s * RB, 16), RB)
+
+    def ins(s):
+        return (pltpu.make_async_copy(dwt_hbm.at[rows(s), :], tb.at[s % 2], isem.at[0, s % 2]),
+                pltpu.make_async_copy(dx_hbm.at[rows(s), :], db.at[s % 2], isem.at[1, s % 2]))
+
+    def outs(s):
+        return (pltpu.make_async_copy(tb.at[s % 2], dw_hbm.at[0, 2, rows(s), :], esem.at[0, s % 2]),
+                pltpu.make_async_copy(db.at[s % 2], dxo_hbm.at[rows(s), :], esem.at[1, s % 2]))
+
+    def xq(k):
+        return pltpu.make_async_copy(x_hbm.at[:, k * 1024:(k + 1) * 1024], xs.at[:, k * 1024:(k + 1) * 1024], xsem.at[k])
+
+    def turn_v():
+        for a, vo in enumerate((v1o_ref, v3o_ref, v2o_ref)):
+            vo[...] = v_ref[a].T
+
+    def turn_g():
+        r = pl.ds(pl.multiple_of(s // 2 * 128, 128), 128)
+        for k in range(3):
+            gt[k, r, :] = (sg_ref[0, k].astype(F32) + sg_ref[1, k].astype(F32)).T
 
     @pl.when(s >= 2)
     def _():
         out(s - 2).wait()
 
-    def main():
-        dxo_ref[...] = dx_ref[...]
-        for a, vo in enumerate((v1o_ref, v3o_ref, v2o_ref)):
-            vo[...] = v_ref[a].T
-        ob[s % 2] = dotf(x_ref[...], h3_ref[0], NT)
-
-    @pl.when(s % 2 == 0)
+    @pl.when(s == 0)
     def _():
-        rows = pl.ds(pl.multiple_of(s // 2 * 128, 128), 128)
-        for k in range(3):
-            gt[k, rows, :] = (sg_ref[0, k].astype(F32) + sg_ref[1, k].astype(F32)).T
-        main()
+        for k in range(4):
+            xq(k).start()
+        for cp in ins(0):
+            cp.start()
+        turn_g()
+        turn_v()
+        for k in range(4):
+            xq(k).wait()
+            kq = slice(k * 1024, (k + 1) * 1024)
+            part = dotf(xs[:, kq], h3_ref[0, :, kq], NT)
+            ob[0] = part if k == 0 else ob[0] + part
+
+    @pl.when((s > 0) & (s % 2 == 0))
+    def _():
+        turn_g()
+        turn_v()
+        ob[0] = dotf(xs[...], h3_ref[0], NT)
 
     @pl.when(s % 2 == 1)
     def _():
-        main()
+        turn_v()
+        ob[1] = dotf(xs[...], h3_ref[0], NT)
 
     out(s).start()
-    third(s).wait()
+    for cp in ins(s):
+        cp.wait()
+    for cp in outs(s):
+        cp.start()
+
+    @pl.when(s > 0)
+    def _():
+        for cp in outs(s - 1):
+            cp.wait()
+
+    @pl.when(s < 9)
+    def _():
+        for cp in ins(s + 1):
+            cp.start()
 
     @pl.when(s == 9)
     def _():
         dn_ref[...] = gt[:, pl.ds(pl.multiple_of(c * SH, 8), SH), :]
         out(8).wait()
         out(9).wait()
+        for cp in outs(9):
+            cp.wait()
 
 
 def run_grad(x, h3, dwt, dx, v, sg):
-    one = pl.Buffered(1)
-    dxs = pl.BlockSpec((D // 10, T), lambda s: (s, 0))
+    hbm = pl.BlockSpec(memory_space=pltpu.MemorySpace.HBM)
     vs = pl.BlockSpec((D, 256), lambda s: (0, s))
+    dma = pltpu.SemaphoreType.DMA
     return pl.pallas_call(
         grad_kernel,
         grid=(10,),
         out_shape=(jax.ShapeDtypeStruct((1, 3, D, F), F32), jax.ShapeDtypeStruct((D, T), BF16),
                    jax.ShapeDtypeStruct((D, F), BF16), jax.ShapeDtypeStruct((D, F), BF16),
                    jax.ShapeDtypeStruct((D, F), BF16), jax.ShapeDtypeStruct((3, SH, D), F32)),
-        in_specs=[pl.BlockSpec((D, T), lambda s: (0, 0), pipeline_mode=one),
-                  pl.BlockSpec((1, 512, T), lambda s: (s // 5, s % 5, 0)),
-                  pl.BlockSpec((D // 10, F), lambda s: (s, 0)), dxs,
+        in_specs=[hbm, pl.BlockSpec((1, 512, T), lambda s: (s // 5, s % 5, 0)), hbm, hbm,
                   pl.BlockSpec((3, 256, D), lambda s: (0, s, 0)),
                   pl.BlockSpec((2, 3, D, 128), lambda s: (0, 0, 0, s // 2))],
-        out_specs=(pl.BlockSpec(memory_space=pltpu.MemorySpace.HBM), dxs, vs, vs, vs,
-                   pl.BlockSpec((3, SH, D), lambda s: (0, 0, 0), pipeline_mode=one)),
-        scratch_shapes=[pltpu.VMEM((2, D, 512), F32), pltpu.VMEM((3, CH, D), F32),
-                        pltpu.SemaphoreType.DMA((2,)), pltpu.SemaphoreType.DMA],
+        out_specs=(hbm, hbm, vs, vs, vs,
+                   pl.BlockSpec((3, SH, D), lambda s: (0, 0, 0), pipeline_mode=pl.Buffered(1))),
+        scratch_shapes=[pltpu.VMEM((D, T), BF16), pltpu.VMEM((2, D, 512), F32), pltpu.VMEM((3, CH, D), F32),
+                        pltpu.VMEM((2, RB, F), F32), pltpu.VMEM((2, RB, T), BF16),
+                        dma((4,)), dma((2,)), dma((2, 2)), dma((2, 2))],
         compiler_params=pltpu.CompilerParams(vmem_limit_bytes=64_000_000),
         cost_estimate=pl.CostEstimate(flops=4 * T * D * F, bytes_accessed=150_000_000, transcendentals=0),
     )(x, h3, dwt, dx, v, sg)

time: 243 us -> 235 us (0.967)
  Pallas kernels: 242 us -> 234 us
    pallas_call x1, Pallas kernels: 183 us -> 175 us  [run_step(): pl.pallas_call(step_kernel, out_shape=(out(2, F, T), out(D, F, dtype=F32)...]
where the time goes in v4:
time: 235 us
  Pallas kernels  234 us (100%)
    pallas_call x1, Pallas kernels, run_step(): pl.pallas_call(step_kernel, out_shape=(out(2, F, T), out(D, F, dtype=F32)...  175 us
    pallas_call x1, Pallas kernels, run_grad(): pl.pallas_call(grad_kernel, grid=(10,), out_shape=(jax.ShapeDtypeStruct((...  58.9 us

profile of v4, /device:TPU:0, one launch (start us, length us, event | category | flops | bytes accessed | tf_op | source)
XLA Modules:
  0.0 234.7 jit_solution(15553391880712115849)
XLA Ops:
  0.6 175.0 %shard_map.136 = (bf16[2,2560,4096]{2,1,0:T(8,128)(2,1)}, f32[960,2560]{1,0:T(8,128)}, bf16[960,4096]{1,0:T(8,128)(2,1)}, bf16[3,2560,960]{2,1,0:T(8,128)(2,1)},...) custom-call(bf16[960,4096]{1,0:T(8,128)(2,1)} %bitcast.12, ...), custom_call_target="tpu_custom_call" | custom-call | flops 120795955200 | bytes 200000000 | tf_op jit(solution)/shard_map/pallas_call | solution.py:537
  175.6 58.9 %shard_map.137 = (f32[1,3,960,2560]{3,2,1,0:T(8,128)}, bf16[960,4096]{1,0:T(8,128)(2,1)}, bf16[960,2560]{1,0:T(8,128)(2,1)}, bf16[960,2560]{1,0:T(8,128)(2,1)}, ...) custom-call(bf16[960,4096]{1,0:T(8,128)(2,1)} %bitcast.13, bf16[2,2560,4096]{2,1,0:T(8,128)(2,1)} %get-tuple-element.17.h3_ref, ...), custom_call_target="tpu_custom_call" | custom-call | flops 40265318400 | bytes 150000000 | tf_op jit(solution)/shard_map/pallas_call | solution.py:652

commit v5 on v4

--- a/solution.py
+++ b/solution.py
@@ -38,8 +38,8 @@
 
 def step_kernel(x_hbm, dy_hbm, w1_hbm, w3_hbm, w2_hbm, v1_hbm, v3_hbm, v2_hbm, g_hbm,
                 h3_hbm, dw_hbm, dx_hbm, v_out, sg, r1, pp, rx, ry, rx2, ry2, sx, sy,
-                x_v, dy_v, acc, w_v, wt, hbuf, h_v, dacc, gin1, gout1, gin2, rin, gout2, ab, ob,
-                lsem, xl, hsem, xsem, wsem, send, recv, g1l, g1s, g1r, g2l, gps, gpr, abl, obs, gms, gmr, zs, zr):
+                x_v, dy_v, acc, w_v, wt, hbuf, h_v, dacc, gin2, rin, gout2, ab, ob,
+                lsem, xl, hsem, xsem, wsem, send, recv, g1s, g1r, g2l, gps, gpr, abl, obs, gms, gmr, zs, zr):
     z = lax.axis_index('dp')
     y = lax.axis_index('col')
     fs = lax.axis_index('fsdp')
@@ -134,12 +134,9 @@
     def half(h):
         return pl.ds(pl.multiple_of(h * HR, 16), HR)
 
-    def g1_load(u):
+    def g1_send(u):
         k, _, cq = unit(u)
-        return pltpu.make_async_copy(g_hbm.at[k, half(1 - c), cq], gin1, g1l)
-
-    def g1_send(u):
-        return rdma(gout1, r1.at[u], g1s, g1r.at[u], partner)
+        return rdma(g_hbm.at[k, half(1 - c), cq], r1.at[u], g1s.at[u], g1r.at[u], partner)
 
     def g2_loads(u):
         k, _, cq = unit(u)
@@ -156,17 +153,6 @@
     def py(k, m):
         return rdma(pp.at[4 * k + 2 * m, pl.ds(QR, QR), :], ry.at[k, m], gps.at[1, k, m], gpr.at[1, k, m], ynbr)
 
-    def g_stage1(u):
-        g1_load(u).wait()
-
-        for r in range(0, HR, 48):
-            gout1[r:r + 48, :] = gin1[r:r + 48, :].astype(BF16)
-        g1_send(u).start()
-
-        @pl.when(u < 11)
-        def _():
-            g1_load(u + 1).start()
-
     def g_sends(u):
         g2_out(u).wait()
         k = u // 3
@@ -189,7 +175,7 @@
             cp.wait()
 
         for r in range(0, HR, 48):
-            gout2[r:r + 48, :] = (gin2[r:r + 48, :].astype(BF16).astype(F32) + rin[r:r + 48, :].astype(F32)).astype(BF16)
+            gout2[r:r + 48, :] = (gin2[r:r + 48, :].astype(BF16).astype(F32) + rin[r:r + 48, :].astype(BF16).astype(F32)).astype(BF16)
         g2_out(u).start()
 
         @pl.when(u < 11)
@@ -264,7 +250,6 @@
 
     for cp in lw + lx(0):
         cp.start()
-    g1_load(0).start()
     bar = pltpu.get_barrier_semaphore()
     for dev in (partner, xnbr, ynbr, znbr):
         pl.semaphore_signal(bar, inc=1, device_id=dev, device_id_type=MESH)
@@ -284,15 +269,12 @@
         j = n // NI
         i = n % NI
 
-        @pl.when((n > 0) & (n <= 12))
-        def _():
-            g1_send(n - 1).wait_send()
-
         @pl.when(n <= S2 + 12)
         def _():
-            @pl.when(n < 12)
+            @pl.when(n == 0)
             def _():
-                g_stage1(n)
+                for u in range(12):
+                    g1_send(u).start()
 
             @pl.when(n == S2 - 1)
             def _():
@@ -516,7 +498,7 @@
         z_fwd(k).wait_recv()
     gvb.recv('dx', 'dy', 'dd')
     gva.recv('dx', 'dy', 'dd')
-    for cp in pw + pv:
+    for cp in pw + pv + [g1_send(u) for u in range(12)]:
         cp.wait_send()
     for g in (gw, gva, gvb):
         g.sent()
@@ -537,7 +519,7 @@
     return pl.pallas_call(
         step_kernel,
         out_shape=(out(2, F, T), out(D, F, dtype=F32), out(D, T), out(3, F, D), out(2, 3, D, CH),
-                   out(12, HR, CH), out(12, HR, CH), out(3, 2, QR, CH), out(3, 2, QR, CH),
+                   out(12, HR, CH, dtype=F32), out(12, HR, CH), out(3, 2, QR, CH), out(3, 2, QR, CH),
                    out(3, QR, CH), out(3, QR, CH), out(3, QR, CH), out(3, QR, CH)),
         in_specs=[hbm] * 9,
         out_specs=(hbm,) * 13,
@@ -545,11 +527,10 @@
             pltpu.VMEM((D, T), BF16), pltpu.VMEM((D, T), BF16), pltpu.VMEM((D, T), F32),
             pltpu.VMEM((3, F, D), BF16), pltpu.VMEM((D, 2 * CH), BF16),
             pltpu.VMEM((2, 2 * CH, TM), BF16), pltpu.VMEM((CH, TM), BF16), pltpu.VMEM((D, CH), F32),
-            pltpu.VMEM((HR, CH), F32), pltpu.VMEM((HR, CH), BF16),
-            pltpu.VMEM((HR, CH), F32), pltpu.VMEM((HR, CH), BF16), pltpu.VMEM((HR, CH), BF16),
+            pltpu.VMEM((HR, CH), F32), pltpu.VMEM((HR, CH), F32), pltpu.VMEM((HR, CH), BF16),
             pltpu.VMEM((6, QR, CH), BF16), pltpu.VMEM((2, QR, CH), BF16),
             dma((6,)), dma((2, NI)), dma((2, 2)), dma, dma, dma((84,)), dma((84,)),
-            dma, dma, dma((12,)), dma((3,)), dma((2, 3, 2)), dma((2, 3, 2)),
+            dma((12,)), dma((12,)), dma((3,)), dma((2, 3, 2)), dma((2, 3, 2)),
             dma((6,)), dma((2,)), dma((2, 3)), dma((2, 3)), dma((3, 3)), dma((3, 3)),
         ],
         compiler_params=pltpu.CompilerParams(collective_id=0, has_side_effects=True,

time: 235 us -> 235 us (level)
  no operation moved by 1% of the time
where the time goes in v5:
time: 235 us
  Pallas kernels  234 us (100%)
    pallas_call x1, Pallas kernels, run_step(): pl.pallas_call(step_kernel, out_shape=(out(2, F, T), out(D, F, dtype=F32)...  175 us
    pallas_call x1, Pallas kernels, run_grad(): pl.pallas_call(grad_kernel, grid=(10,), out_shape=(jax.ShapeDtypeStruct((...  58.9 us

profile of v5, /device:TPU:0, one launch (start us, length us, event | category | flops | bytes accessed | tf_op | source)
XLA Modules:
  0.0 234.9 jit_solution(7259273846146989161)
XLA Ops:
  0.6 175.2 %shard_map.136 = (bf16[2,2560,4096]{2,1,0:T(8,128)(2,1)}, f32[960,2560]{1,0:T(8,128)}, bf16[960,4096]{1,0:T(8,128)(2,1)}, bf16[3,2560,960]{2,1,0:T(8,128)(2,1)},...) custom-call(bf16[960,4096]{1,0:T(8,128)(2,1)} %bitcast.12, ...), custom_call_target="tpu_custom_call" | custom-call | flops 120795955200 | bytes 200000000 | tf_op jit(solution)/shard_map/pallas_call | solution.py:519
  175.8 58.9 %shard_map.137 = (f32[1,3,960,2560]{3,2,1,0:T(8,128)}, bf16[960,4096]{1,0:T(8,128)(2,1)}, bf16[960,2560]{1,0:T(8,128)(2,1)}, bf16[960,2560]{1,0:T(8,128)(2,1)}, ...) custom-call(bf16[960,4096]{1,0:T(8,128)(2,1)} %bitcast.13, bf16[2,2560,4096]{2,1,0:T(8,128)(2,1)} %get-tuple-element.17.h3_ref, ...), custom_call_target="tpu_custom_call" | custom-call | flops 40265318400 | bytes 150000000 | tf_op jit(solution)/shard_map/pallas_call | solution.py:633

commit v6 on v5

--- a/solution.py
+++ b/solution.py
@@ -26,7 +26,7 @@
 QR = HR // 2
 RB = D // 10
 S2 = 2
-G_AT = (9, 12, 15, 18, 21, 24)
+G_AT = (10, 11, 15, 18, 21, 24)
 
 NN = (((1,), (0,)), ((), ()))
 NT = (((1,), (1,)), ((), ()))
@@ -334,7 +334,7 @@
             gw.recv('xf', 'yf')
             gw.start('zd0', 'zd1')
 
-        @at(11)
+        @at(12)
         def _():
             gva.recv('x0')
             gva.start('yf', 'zx0')
@@ -353,58 +353,64 @@
         @at(16)
         def _():
             gw.recv('dy')
+
+        @at(17)
+        def _():
             gva.recv('xf', 'yf')
             gva.start('zd0', 'zd1')
-            gvb.start('x0', 'y1')
-
-        @at(19)
+
+        @at(18)
         def _():
             gw.recv('zd0', 'zd1')
             gw.start('dd')
+
+        @at(19)
+        def _():
+            gvb.start('x0', 'y1')
+
+        @at(20)
+        def _():
             gvb.start('x1', 'y0')
 
-        @at(20)
+        @at(21)
         def _():
             gva.recv('zx0', 'zx1', 'zy0', 'zy1')
             gva.start('dx', 'dy')
             gva.recv('zd0', 'zd1')
             gva.start('dd')
 
-        @at(23)
+        @at(24)
+        def _():
+            gw.recv('dd')
+            z_sends(0)[0].wait_recv()
+            z_fwd(0).start()
+
+        @at(25)
         def _():
             gvb.recv('x0')
             gvb.start('yf')
             gvb.recv('y1')
             gvb.start('xf')
 
-        @at(24)
-        def _():
-            gw.recv('dd')
-
-        @at(25)
-        def _():
-            z_sends(0)[0].wait_recv()
-            z_fwd(0).start()
-
-        @at(27)
+        @at(28)
+        def _():
+            z_sends(1)[0].wait_recv()
+            z_fwd(1).start()
+
+        @at(29)
         def _():
             gvb.recv('x1', 'y0')
             gvb.start('dx', 'dy')
 
-        @at(28)
-        def _():
-            z_sends(1)[0].wait_recv()
-            z_fwd(1).start()
-
         @at(30)
+        def _():
+            z_sends(2)[0].wait_recv()
+            z_fwd(2).start()
+
+        @at(31)
         def _():
             gvb.recv('xf', 'yf')
             gvb.start('dd')
-
-        @at(31)
-        def _():
-            z_sends(2)[0].wait_recv()
-            z_fwd(2).start()
 
         for e, (k, fin) in zip(G_AT, ((0, 0), (1, 0), (2, 0), (0, 1), (1, 1), (2, 1))):
             at(e + 2)(functools.partial(g_push, k, fin))

time: 235 us -> 235 us (level)
  no operation moved by 1% of the time
where the time goes in v6:
time: 235 us
  Pallas kernels  234 us (100%)
    pallas_call x1, Pallas kernels, run_step(): pl.pallas_call(step_kernel, out_shape=(out(2, F, T), out(D, F, dtype=F32)...  175 us
    pallas_call x1, Pallas kernels, run_grad(): pl.pallas_call(grad_kernel, grid=(10,), out_shape=(jax.ShapeDtypeStruct((...  58.9 us

profile of v6, /device:TPU:0, one launch (start us, length us, event | category | flops | bytes accessed | tf_op | source)
XLA Modules:
  0.0 234.5 jit_solution(14045753440999510638)
XLA Ops:
  0.6 174.8 %shard_map.136 = (bf16[2,2560,4096]{2,1,0:T(8,128)(2,1)}, f32[960,2560]{1,0:T(8,128)}, bf16[960,4096]{1,0:T(8,128)(2,1)}, bf16[3,2560,960]{2,1,0:T(8,128)(2,1)},...) custom-call(bf16[960,4096]{1,0:T(8,128)(2,1)} %bitcast.12, ...), custom_call_target="tpu_custom_call" | custom-call | flops 120795955200 | bytes 200000000 | tf_op jit(solution)/shard_map/pallas_call | solution.py:525
  175.4 58.9 %shard_map.137 = (f32[1,3,960,2560]{3,2,1,0:T(8,128)}, bf16[960,4096]{1,0:T(8,128)(2,1)}, bf16[960,2560]{1,0:T(8,128)(2,1)}, bf16[960,2560]{1,0:T(8,128)(2,1)}, ...) custom-call(bf16[960,4096]{1,0:T(8,128)(2,1)} %bitcast.13, bf16[2,2560,4096]{2,1,0:T(8,128)(2,1)} %get-tuple-element.17.h3_ref, ...), custom_call_target="tpu_custom_call" | custom-call | flops 40265318400 | bytes 150000000 | tf_op jit(solution)/shard_map/pallas_call | solution.py:639
